TPU v7x, 32 devices: a whole 2x2x4 slice. The times are simulated.
32 devices in a mesh: dp: 8 (over z, y), mp: 4 (over x, core).
Axes of the slice: x: 2, y: 2, z: 4, core: 2. Of those that a mesh axis runs over, the one named last changes fastest.
Arguments:
- tokens: bfloat16 [6144, 768], P(('dp', 'mp')), may hold values from -6 to 6
- obs_mask: int32 [96, 64], P(('dp', 'mp')), may hold values 0 or 1
- norm_gains: float32 [5, 768], replicated, may hold values from 0.1 to 1.9
- attn_in: bfloat16 [2, 3, 768, 768], P(None, None, 'dp', 'mp'), may hold values from -0.21875 to 0.21875
- attn_out: bfloat16 [2, 768, 768], P(None, 'mp', 'dp'), may hold values from -0.21875 to 0.21875
- mlp_in: bfloat16 [2, 768, 3072], P(None, 'dp', 'mp'), may hold values from -0.21875 to 0.21875
- mlp_out: bfloat16 [2, 3072, 768], P(None, 'mp', 'dp'), may hold values from -0.109375 to 0.109375
- embodiment: int32 [96, 1], P('dp'), may hold values from 0 to 24; in each aligned block of 12 rows (0 to 11, 12 to 23, ...) no two rows name the same one
- levels: int32 [96, 2], P('dp'), may hold values from 0 to 19
- actions: bfloat16 [96, 2, 56], P('dp'), may hold values from -1 to 1
- noise: bfloat16 [96, 2, 56], P('dp'), may hold values from -5 to 5
- action_dims: int32 [25], replicated, may hold values from 7 to 14
- head_read: bfloat16 [32, 768, 256], P('dp'), may hold values from -0.21875 to 0.21875
- head_act: bfloat16 [32, 56, 256], P('dp'), may hold values from -0.75 to 0.75
- time_table: bfloat16 [32, 20, 256], P('dp'), may hold values from -5 to 5
- block_in: bfloat16 [32, 256, 256], P('dp'), may hold values from -0.375 to 0.375
- block_out: bfloat16 [32, 256, 256], P('dp'), may hold values from -0.375 to 0.375
- head_out: bfloat16 [32, 256, 56], P('dp'), may hold values from -0.375 to 0.375
Outputs:
- readout_grad: bfloat16 [96, 2, 768], P(('dp', 'mp'))
- grad_read: float32 [32, 768, 256], P('dp', 'mp')
- grad_act: float32 [32, 56, 256], P('dp')
- grad_time: float32 [32, 20, 256], P('dp')
- grad_block_in: float32 [32, 256, 256], P('dp')
- grad_block_out: float32 [32, 256, 256], P('dp')
- grad_head_out: float32 [32, 256, 56], P('dp')
Inputs may be any that keep to these rules, and one draw needn't show every extreme that they name: Within each aligned block of 12 samples (those of one dp index) no embodiment appears twice; every embodiment appears in some block.
All inputs are finite; a program needn't handle non-finite values. No bound on the sum of `obs_mask` on one device may be relied on, other than what follows from the above.
Results may differ from a plain program's by a relative error of at most 0.024.
Values may be sent and summed in bfloat16 or wider, within the bound.
A program may use at most 64 MiB of HBM per device.

v0:
```python
import functools
import math

import jax
import jax.numpy as jnp
from jax import lax
from jax.experimental import pallas as pl
from jax.experimental.pallas import tpu as pltpu
from jax.sharding import PartitionSpec as P

HDIM = 64
EMB = 25
READ = 2
LEVELS = 20
ADIM_MAX = 14

norm_eps = 1e-05
MESH_ID = pl.DeviceIdType.MESH


def normalize(values, scale_gain):
    center = values - jnp.mean(values, axis=-1, keepdims=True)
    spread = jnp.mean(center * center, axis=-1, keepdims=True)
    return center * lax.rsqrt(spread + norm_eps) * scale_gain


def plan():
    steps_up = (jnp.arange(LEVELS, dtype=jnp.float32) + 1.0) / LEVELS
    anchor = math.cos(0.008 / 1.008 * math.pi / 2) ** 2
    return jnp.cos((steps_up + 0.008) / 1.008 * (math.pi / 2)) ** 2 / anchor


def noisy_pair(level_ids, clean, noise_draw, table):
    picked = (level_ids[..., None] == jnp.arange(LEVELS)).astype(jnp.float32)
    kept = jnp.sum(picked * table, axis=-1)[..., None]
    mixed = jnp.sqrt(kept) * clean.astype(jnp.float32) + jnp.sqrt(1.0 - kept) * noise_draw.astype(
        jnp.float32
    )
    return mixed.astype(jnp.bfloat16)


def ring_place(index, size):
    if size % 2:
        return index
    odd = index % 2
    return (1 - odd) * (index // 2) + odd * (size - 1 - index // 2)


def ring_index(place, size):
    if size % 2:
        return place
    back = place // (size // 2)
    return (1 - back) * (2 * place) + back * (2 * (size - 1 - place) + 1)


def ring_parts(rows, tile=16):
    if rows % tile:
        return [(0, rows)]
    return [(start, tile) for start in range(0, rows, tile)]


def ring_step(parts, step, size):
    count = len(parts)
    if size % 2 == 0 and step == size // 2 - 1:
        near = (count + 1) // 2
        pairs = [(0, chunk) for chunk in range(near)], [(1, chunk) for chunk in range(near, count)]
        mixed = []
        for chunk in range(near):
            mixed += [side[chunk] for side in pairs if chunk < len(side)]
        return mixed
    return [(way, chunk) for chunk in range(count) for way in range(2)]


def exchange_kernel(n_dp, n_mp, kinds, *refs):
    count = len(kinds)
    ins, outs = refs[:count], refs[count : 2 * count]
    sems = refs[2 * count :]
    local_sem = sems[-1]
    my_dp, my_mp = lax.axis_index("dp"), lax.axis_index("mp")
    place = ring_place(my_dp, n_dp)

    talk_mp = any(kind in ("split", "cast") for kind in kinds)
    talk_dp = "swap" in kinds
    talk_ring = "ring" in kinds
    barrier = pltpu.get_barrier_semaphore()
    greeted = 0
    if talk_mp:
        for offset in range(1, n_mp):
            pl.semaphore_signal(
                barrier, inc=1, device_id={"mp": (my_mp + offset) % n_mp}, device_id_type=MESH_ID
            )
            greeted += 1
    if talk_dp:
        for offset in range(1, n_dp):
            pl.semaphore_signal(
                barrier, inc=1, device_id={"dp": (my_dp + offset) % n_dp}, device_id_type=MESH_ID
            )
            greeted += 1
    elif talk_ring:
        for way in (1, n_dp - 1):
            pl.semaphore_signal(
                barrier,
                inc=1,
                device_id={"dp": ring_index((place + way) % n_dp, n_dp)},
                device_id_type=MESH_ID,
            )
            greeted += 1
    pl.semaphore_wait(barrier, greeted)

    def ring_copies(item, step):
        source, landing = ins[item], outs[item]
        parts = ring_parts(source.shape[0])
        made = {}
        for way, chunk in ring_step(parts, step, n_dp):
            origin = ring_index((place + (n_dp - step if way == 0 else step)) % n_dp, n_dp)
            target = ring_index((place + (1 if way == 0 else n_dp - 1)) % n_dp, n_dp)
            rows = pl.ds(*parts[chunk])
            spot = landing.at[origin, rows]
            made[way, chunk] = pltpu.make_async_remote_copy(
                src_ref=source.at[rows] if step == 0 else spot,
                dst_ref=spot,
                send_sem=sems[2 * item].at[step, chunk, way],
                recv_sem=sems[2 * item + 1].at[step, chunk, way],
                device_id={"dp": target},
                device_id_type=MESH_ID,
            )
        return made

    rings = [item for item in range(count) if kinds[item] == "ring"]
    flights = {item: ring_copies(item, 0) for item in rings}
    for item in rings:
        for copy in flights[item].values():
            copy.start()
    direct = []
    keeps = []
    for item, kind in enumerate(kinds):
        source, landing = ins[item], outs[item]
        if kind == "ring":
            keeps.append(pltpu.make_async_copy(source, landing.at[my_dp], local_sem.at[item]))
            continue
        size, mine, axis = (n_dp, my_dp, "dp") if kind == "swap" else (n_mp, my_mp, "mp")
        for offset in range(1, size):
            peer = (mine + offset) % size
            copy = pltpu.make_async_remote_copy(
                src_ref=source if kind == "cast" else source.at[peer],
                dst_ref=landing.at[mine],
                send_sem=sems[2 * item].at[offset],
                recv_sem=sems[2 * item + 1].at[offset],
                device_id={axis: peer},
                device_id_type=MESH_ID,
            )
            copy.start()
            direct.append(copy)
        keeps.append(
            pltpu.make_async_copy(
                source if kind == "cast" else source.at[mine], landing.at[mine], local_sem.at[item]
            )
        )
    for keep in keeps:
        keep.start()
    sent = [copy for item in rings for copy in flights[item].values()]
    landed = []
    for step in range(1, n_dp // 2):
        for item in rings:
            following = ring_copies(item, step)
            for key, after in following.items():
                flights[item].pop(key).wait_recv()
                after.start()
            landed += flights[item].values()
            flights[item] = following
            sent += following.values()
    for item in rings:
        landed += flights[item].values()
    for copy in landed:
        copy.wait_recv()
    for copy in direct:
        copy.wait_recv()
    for copy in sent + direct:
        copy.wait_send()
    for keep in keeps:
        keep.wait()


def exchange(ident, *pairs):
    n_dp, n_mp = lax.axis_size("dp"), lax.axis_size("mp")
    kinds = tuple(kind for kind, _ in pairs)
    arrays = [array for _, array in pairs]
    shapes, scratch = [], []
    for kind, array in pairs:
        lead = {"ring": (n_dp,), "cast": (n_mp,), "split": (), "swap": ()}[kind]
        shapes.append(jax.ShapeDtypeStruct(lead + array.shape, array.dtype))
        if kind == "ring":
            slots = (n_dp // 2, len(ring_parts(array.shape[0])), 2)
        else:
            slots = (n_dp if kind == "swap" else n_mp,)
        scratch += [pltpu.SemaphoreType.DMA(slots), pltpu.SemaphoreType.DMA(slots)]
    scratch.append(pltpu.SemaphoreType.DMA((len(pairs),)))
    return pl.pallas_call(
        functools.partial(exchange_kernel, n_dp, n_mp, kinds),
        out_shape=shapes,
        in_specs=[pl.BlockSpec(memory_space=pltpu.VMEM)] * len(pairs),
        out_specs=[pl.BlockSpec(memory_space=pltpu.VMEM)] * len(pairs),
        scratch_shapes=scratch,
        compiler_params=pltpu.CompilerParams(collective_id=ident, has_side_effects=True),
        name="exchange%d" % ident,
    )(*arrays)


def attend(queries, key_rows, value_rows, allowed):
    scores = jnp.einsum(
        "sqhd,skhd->shqk", queries, key_rows, preferred_element_type=jnp.float32
    ) * HDIM ** (-0.5)
    weights = jnp.where(allowed[:, None, :, :], jnp.exp(scores), 0.0)
    shares = (weights / jnp.sum(weights, axis=-1, keepdims=True)).astype(jnp.bfloat16)
    context = jnp.einsum("shqk,skhd->sqhd", shares, value_rows, preferred_element_type=jnp.float32)
    return context.astype(jnp.bfloat16)


def dot32(left, right):
    return jnp.dot(left, right, preferred_element_type=jnp.float32)


def dot_turned(left, right):
    return lax.dot_general(
        left, right, (((1,), (1,)), ((), ())), preferred_element_type=jnp.float32
    )


def added(blocks):
    return jnp.sum(blocks.astype(jnp.float32), axis=0)


def tail(first, target, weight_mask, inner_weight, outer_weight, final_weight):
    highest = lax.Precision.HIGHEST
    active = jax.nn.silu(first).astype(jnp.bfloat16)
    inner = jnp.dot(active, inner_weight, preferred_element_type=jnp.float32, precision=highest)
    second = jax.nn.silu(inner).astype(jnp.bfloat16)
    hidden = first + jnp.dot(
        second, outer_weight, preferred_element_type=jnp.float32, precision=highest
    )
    third = jax.nn.silu(hidden).astype(jnp.bfloat16)
    predicted = jnp.dot(third, final_weight, preferred_element_type=jnp.float32, precision=highest)
    differ = predicted - target
    return 0.5 * jnp.sum(weight_mask * differ * differ)


def head_grads(first, inner_weight, outer_weight, final_weight, target, weight_mask):

    def head_loss(first_in, inner_in, outer_in, final_in):
        return tail(first_in, target, weight_mask, inner_in, outer_in, final_in)

    loss_value, pullback = jax.vjp(head_loss, first, inner_weight, outer_weight, final_weight)
    return pullback(jnp.ones((), jnp.float32))


def on_device(
    tokens,
    obs_mask,
    norm_gains,
    attn_in,
    attn_out,
    mlp_in,
    mlp_out,
    embodiment,
    levels,
    actions,
    noise,
    action_dims,
    head_read,
    head_act,
    time_table,
    block_in,
    block_out,
    head_out,
):
    model = tokens.shape[1]
    act = actions.shape[2]
    width = attn_in.shape[3]
    heads_local = width // HDIM
    samples_local, length = obs_mask.shape
    layer_count = attn_in.shape[0]
    n_mp, n_dp = lax.axis_size("mp"), lax.axis_size("dp")
    my_model, my_owner = lax.axis_index("mp"), lax.axis_index("dp")
    samples_group = samples_local * n_mp
    ident = iter(range(100))

    joined = [
        jnp.concatenate(
            [attn_in[layer, 0], attn_in[layer, 1], attn_in[layer, 2], attn_out[layer].T], axis=1
        )
        for layer in range(layer_count)
    ]
    lowered = [mlp_out[layer].T for layer in range(layer_count)]

    heads_dev = head_read.shape[0]
    slot_count = heads_dev * n_dp
    owners = embodiment[:, 0]
    table = plan()
    onto = (jnp.arange(slot_count)[:, None] == owners[None, :]).astype(jnp.bfloat16)
    spread_rows = jnp.einsum("es,rq->ersq", onto, jnp.eye(READ, dtype=jnp.bfloat16)).reshape(
        slot_count * READ, samples_group * READ
    )
    small = jnp.concatenate(
        [
            noisy_pair(levels, actions, noise, table),
            noise,
            (levels + 1)[..., None].astype(jnp.bfloat16),
        ],
        axis=-1,
    ).reshape(samples_group * READ, 2 * act + 1)
    small = jnp.pad(small, ((0, 0), (0, -small.shape[1] % 128)))
    small = dot32(spread_rows, small).astype(jnp.bfloat16)
    small = small.reshape(n_dp, heads_dev * READ, small.shape[1])

    residual = tokens.astype(jnp.float32)
    wide = None
    allowed = None
    mask_group = None
    got_small = None
    position = jnp.arange(length)
    for layer in range(layer_count):
        final = layer == layer_count - 1
        normed = normalize(residual, norm_gains[2 * layer]).astype(jnp.bfloat16)
        if layer == 0:
            sends = [("cast", normed), ("cast", obs_mask), ("swap", small), ("ring", joined[0])]
        else:
            sends = [("cast", normed)]
        if final:
            ends = residual.reshape(samples_local, length, model)[:, length - READ :, :]
            sends += [("cast", ends), ("ring", mlp_in[layer]), ("ring", lowered[layer])]
        got = list(exchange(next(ident), *sends))
        gathered = got.pop(0).reshape(-1, model)
        if layer == 0:
            mask_group = got.pop(0).reshape(samples_group, length)
            got_small = got.pop(0)
            wide = got.pop(0).reshape(model, -1)
            visible = (mask_group == 1) & (position < length - READ)[None, :]
            itself = position[:, None] == position[None, :]
            allowed = visible[:, None, :] | itself[None, :, :]
        if final:
            ends = got.pop(0).reshape(samples_group * READ, model)
            upper = got.pop(0).reshape(model, -1)
            lower = got.pop(0).reshape(model, -1)
            asking = gathered.reshape(samples_group, length, model)[:, length - READ :, :]
            queries = dot32(asking.reshape(-1, model), wide[:, :width]).astype(jnp.bfloat16)
            queries = queries.reshape(samples_group, READ, heads_local, HDIM)
            both = dot32(gathered, wide[:, width : 3 * width]).astype(jnp.bfloat16)
            keys_at = both[:, :width].reshape(samples_group, length, heads_local, HDIM)
            values_at = both[:, width:].reshape(samples_group, length, heads_local, HDIM)
            context = attend(queries, keys_at, values_at, allowed[:, length - READ :, :])
            partial_value = dot_turned(context.reshape(-1, width), wide[:, 3 * width :])
            (terms,) = exchange(next(ident), ("cast", partial_value.astype(jnp.bfloat16)))
            ends = ends + added(terms)
            normed = normalize(ends, norm_gains[2 * layer + 1]).astype(jnp.bfloat16)
            hidden = jax.nn.gelu(dot32(normed, upper), approximate=True).astype(jnp.bfloat16)
            partial_value = dot_turned(hidden, lower)
            (terms,) = exchange(next(ident), ("cast", partial_value.astype(jnp.bfloat16)))
            ends = ends + added(terms)
            break
        projected = dot32(gathered, wide[:, : 3 * width]).astype(jnp.bfloat16)
        split = [
            projected[:, part * width : (part + 1) * width].reshape(
                samples_group, length, heads_local, HDIM
            )
            for part in range(3)
        ]
        context = attend(split[0], split[1], split[2], allowed).reshape(-1, width)
        partial_value = dot_turned(context, wide[:, 3 * width :]).astype(jnp.bfloat16)
        terms, upper = exchange(
            next(ident),
            ("split", partial_value.reshape(n_mp, -1, model)),
            ("ring", mlp_in[layer]),
        )
        residual = residual + added(terms)
        normed = normalize(residual, norm_gains[2 * layer + 1]).astype(jnp.bfloat16)
        gathered, lower = exchange(next(ident), ("cast", normed), ("ring", lowered[layer]))
        raised = dot32(gathered.reshape(-1, model), upper.reshape(model, -1))
        hidden = jax.nn.gelu(raised, approximate=True).astype(jnp.bfloat16)
        partial_value = dot_turned(hidden, lower.reshape(model, -1)).astype(jnp.bfloat16)
        terms, wide = exchange(
            next(ident),
            ("split", partial_value.reshape(n_mp, -1, model)),
            ("ring", joined[layer + 1]),
        )
        wide = wide.reshape(model, -1)
        residual = residual + added(terms)

    readouts = normalize(ends, norm_gains[2 * layer_count]).astype(jnp.bfloat16)
    send = dot32(spread_rows, readouts).astype(jnp.bfloat16)
    (got_features,) = exchange(
        next(ident), ("swap", send.reshape(n_dp, heads_dev * READ, model))
    )

    def by_head(values):
        values = values.reshape(n_dp, heads_dev, READ, values.shape[-1])
        return jnp.moveaxis(values, 1, 0).reshape(heads_dev, n_dp * READ, values.shape[-1])

    head_features = by_head(got_features)
    head_small = by_head(got_small)
    head_noisy = head_small[..., :act]
    head_target = head_small[..., act : 2 * act].astype(jnp.float32)
    head_levels = head_small[..., 2 * act].astype(jnp.int32) - 1
    head_onehot = (head_levels[..., None] == jnp.arange(LEVELS)).astype(jnp.bfloat16)
    slot_ids = my_owner * heads_dev + jnp.arange(heads_dev)
    dims_here = jnp.sum(
        jnp.where(jnp.arange(EMB)[None, :] == slot_ids[:, None], action_dims[None, :], 0), axis=1
    )
    column = jnp.arange(act) % ADIM_MAX
    weight_mask = (head_levels >= 0).astype(jnp.float32)[..., None] * (
        column[None, None, :] < dims_here[:, None, None]
    ).astype(jnp.float32)
    others = jnp.einsum("hna,hac->hnc", head_noisy, head_act, preferred_element_type=jnp.float32)
    others = others + jnp.einsum(
        "hnl,hlc->hnc", head_onehot, time_table, preferred_element_type=jnp.float32
    )
    first = (
        jnp.einsum("hnd,hdc->hnc", head_features, head_read, preferred_element_type=jnp.float32)
        + others
    )
    grad_first, grad_inner, grad_outer, grad_final = jax.vmap(head_grads)(
        first,
        block_in.astype(jnp.float32),
        block_out.astype(jnp.float32),
        head_out.astype(jnp.float32),
        head_target,
        weight_mask,
    )
    grad_bf = grad_first.astype(jnp.bfloat16)
    backward = jnp.einsum(
        "hnc,hdc->hnd", grad_bf, head_read, preferred_element_type=jnp.float32
    ).astype(jnp.bfloat16)
    backward = jnp.moveaxis(backward.reshape(heads_dev, n_dp, READ, model), 0, 1)
    (arrived,) = exchange(
        next(ident), ("swap", backward.reshape(n_dp, heads_dev * READ, model))
    )
    mine = lax.dynamic_slice_in_dim(
        spread_rows, my_model * (samples_local * READ), samples_local * READ, 1
    )
    returned = lax.dot_general(
        mine,
        arrived.reshape(slot_count * READ, model),
        (((0,), (0,)), ((), ())),
        preferred_element_type=jnp.float32,
    ).astype(jnp.bfloat16)
    feature_width = model // n_mp
    own_features = lax.dynamic_slice_in_dim(
        head_features, my_model * feature_width, feature_width, 2
    )
    grad_readin = jnp.einsum(
        "hnd,hnc->hdc", own_features, grad_bf, preferred_element_type=jnp.float32
    )
    grad_actin = jnp.einsum("hna,hnc->hac", head_noisy, grad_bf, preferred_element_type=jnp.float32)
    grad_timein = jnp.einsum(
        "hnl,hnc->hlc", head_onehot, grad_bf, preferred_element_type=jnp.float32
    )
    return (
        returned.reshape(samples_local, READ, model),
        grad_readin,
        grad_actin,
        grad_timein,
        grad_inner,
        grad_outer,
        grad_final,
    )


def solution(mesh):
    placed = (
        P(("dp", "mp"), None),
        P(("dp", "mp"), None),
        P(),
        P(None, None, "dp", "mp"),
        P(None, "mp", "dp"),
        P(None, "dp", "mp"),
        P(None, "mp", "dp"),
        P("dp", None),
        P("dp", None),
        P("dp", None, None),
        P("dp", None, None),
        P(),
        P("dp", None, None),
        P("dp", None, None),
        P("dp", None, None),
        P("dp", None, None),
        P("dp", None, None),
        P("dp", None, None),
    )
    return jax.shard_map(
        on_device,
        mesh=mesh,
        in_specs=placed,
        out_specs=(
            P(("dp", "mp"), None, None),
            P("dp", "mp", None),
            P("dp", None, None),
            P("dp", None, None),
            P("dp", None, None),
            P("dp", None, None),
            P("dp", None, None),
        ),
        check_vma=False,
    )
```

profile of v0, /device:TPU:0, one launch (start us, length us, event | category | flops | bytes accessed | tf_op | source)
XLA Modules:
  0.0 218.8 jit_solution(5256671850950722257)
XLA Ops:
  0.7 1.0 select_reduce_fusion
  3.1 1.1 convert_reduce_fusion.2
  4.2 1.2 fusion.28
  7.3 0.8 add_convert_fusion
  8.1 1.6 slice_reduce_fusion
  9.7 0.8 fusion.124
  11.1 0.8 fusion.24.refs_2_
  11.9 0.9 fusion.30.refs_0_
  12.9 0.8 pad_maximum_fusion
  15.2 24.5 %exchange0.1 = (bf16[4,192,768]{2,1,0:T(8,128)(2,1)}, s32[4,3,64]{2,1,0:T(4,128)}, bf16[8,8,128]{2,1,0:T(8,128)(2,1)}, bf16[8,96,768]{2,1,0:T(8,128)(2,1)}) custom-call(bf16[192,768]{1,0:T(8,128)(2,1)} %fusion.30.refs_0_, s32[3,64]{1,0:T(4,128)} %refs_1_.1, bf16[8,8,128]{2,1,0:T(8,128)(2,1)} %fusion.24.refs_2_, bf16[96,768]{1,0:T(8,128)(2,1)} %get-tuple-element.86.refs_3_), custom_call_target="tpu_custom_call" | custom-call | tf_op jit(solution)/shard_map/exchange0/pallas_call | solution.py:198
  40.4 2.5 %convolution_convert_fusion.2 = bf16[768,576]{0,1:T(8,128)(2,1)S(1)} fusion(bf16[768,768]{1,0:T(8,128)(2,1)} %bitcast.145, bf16[768,768]{1,0:T(8,128)(2,1)} %bitcast.136), kind=kOutput, calls=%fused_computation.13 | convolution fusion | flops 679919616 | bytes 3047424 | tf_op jit(solution)/shard_map/dot_general | solution.py:220
  42.9 0.8 fusion.72
  46.1 0.8 copy.74
  47.4 1.3 reshape.355
  48.7 1.3 reshape.354
  50.1 2.9 %fusion.9 = f32[12,3,64,64]{2,3,1,0:T(8,128)} fusion(bf16[12,64,3,64]{1,0,3,2:T(8,128)(2,1)} %reshape.355, bf16[12,64,3,64]{1,0,3,2:T(8,128)(2,1)} %reshape.354, pred[12,64,64]{1,2,0:T(8,128)(4,1)S(1)} %copy-done.7), kind=kOutput, calls=%fused_computation.16 | convolution fusion | flops 19169280 | bytes 1228800 | tf_op jit(solution)/shard_map/sqhd,skhd->shqk/dot_general | solution.py:210
  53.0 2.9 %fusion.10 = bf16[12,64,3,64]{1,3,2,0:T(8,128)(2,1)} fusion(f32[12,3,64,64]{2,3,1,0:T(8,128)} %fusion.9, bf16[12,64,3,64]{1,0,3,2:T(8,128)(2,1)S(1)} %reshape.353), kind=kOutput, calls=%fused_computation.19 | convolution fusion | flops 19319104 | bytes 1179648 | tf_op jit(solution)/shard_map/shqk,skhd->sqhd/dot_general | solution.py:215
  55.9 1.5 copy.72
  57.8 2.7 %convolution_convert_fusion.1 = bf16[768,768]{1,0:T(8,128)(2,1)} fusion(bf16[768,192]{0,1:T(8,128)(2,1)S(1)} %reshape.356, bf16[768,768]{1,0:T(8,128)(2,1)} %bitcast.137), kind=kOutput, calls=%fused_computation.12 | convolution fusion | flops 227082240 | bytes 1867776 | tf_op jit(solution)/shard_map/dot_general | solution.py:224
  60.5 19.6 %exchange1.1 = (bf16[4,192,768]{2,1,0:T(8,128)(2,1)}, bf16[8,96,768]{2,1,0:T(8,128)(2,1)}) custom-call(bf16[4,192,768]{2,1,0:T(8,128)(2,1)} %bitcast.120, bf16[96,768]{1,0:T(8,128)(2,1)} %get-tuple-element.75.refs_1_), custom_call_target="tpu_custom_call" | custom-call | tf_op jit(solution)/shard_map/exchange1/pallas_call | solution.py:198
  80.1 1.5 convert_reduce_fusion.1
  82.3 0.9 multiply_convert_fusion.1.refs_0_
  83.2 19.3 %exchange2.1 = (bf16[4,192,768]{2,1,0:T(8,128)(2,1)}, bf16[8,96,768]{2,1,0:T(8,128)(2,1)}) custom-call(bf16[192,768]{1,0:T(8,128)(2,1)} %multiply_convert_fusion.1.refs_0_, bf16[96,768]{1,0:T(8,128)(2,1)} %get-tuple-element.73.refs_1_), custom_call_target="tpu_custom_call" | custom-call | tf_op jit(solution)/shard_map/exchange2/pallas_call | solution.py:198
  102.4 5.2 %convolution_convert_fusion = bf16[768,768]{1,0:T(8,128)(2,1)} fusion(bf16[768,768]{1,0:T(8,128)(2,1)} %bitcast.147, bf16[768,768]{1,0:T(8,128)(2,1)} %bitcast.146, bf16[768,768]{1,0:T(8,128)(2,1)} %bitcast.144), kind=kOutput, calls=%fused_computation.11 | convolution fusion | flops 1817837568 | bytes 4718592 | tf_op jit(solution)/shard_map/dot_general | solution.py:224
  107.7 19.8 %exchange3.1 = (bf16[4,192,768]{2,1,0:T(8,128)(2,1)}, bf16[8,96,768]{2,1,0:T(8,128)(2,1)}) custom-call(bf16[4,192,768]{2,1,0:T(8,128)(2,1)} %bitcast.123, bf16[96,768]{1,0:T(8,128)(2,1)} %get-tuple-element.87.refs_1_), custom_call_target="tpu_custom_call" | custom-call | tf_op jit(solution)/shard_map/exchange3/pallas_call | solution.py:198
  127.4 1.5 convert_reduce_fusion
  129.9 0.9 multiply_convert_fusion.refs_0_
  130.8 30.2 %exchange4.1 = (bf16[4,192,768]{2,1,0:T(8,128)(2,1)}, f32[4,3,2,768]{3,2,1,0:T(2,128)}, bf16[8,96,768]{2,1,0:T(8,128)(2,1)}, bf16[8,96,768]{2,1,0:T(8,128)(2,1)}) custom-call(bf16[192,768]{1,0:T(8,128)(2,1)} %multiply_convert_fusion.refs_0_, f32[3,2,768]{2,1,0:T(2,128)} %slice.138.refs_1_, bf16[96,768]{1,0:T(8,128)(2,1)} %get-tuple-element.74.refs_2_, ...), custom_call_target="tpu_custom_call" | custom-call | tf_op jit(solution)/shard_map/exchange4/pallas_call | solution.py:198
  161.0 1.0 slice.142
  162.3 2.1 convolution_convert_fusion.3
  165.4 1.4 reshape.365
  166.7 1.7 fusion.23
  168.6 1.9 convolution_convert_fusion.8.refs_0_
  170.5 5.7 %exchange5.1 = bf16[4,24,768]{2,1,0:T(8,128)(2,1)} custom-call(bf16[24,768]{1,0:T(8,128)(2,1)} %convolution_convert_fusion.8.refs_0_), custom_call_target="tpu_custom_call" | custom-call | tf_op jit(solution)/shard_map/exchange5/pallas_call | solution.py:198
  176.2 0.9 convert_reduce_fusion.4
  177.7 2.6 %convolution_convert_fusion.7.refs_0_ = bf16[24,768]{1,0:T(8,128)(2,1)} fusion(bf16[768,768]{1,0:T(8,128)(2,1)} %bitcast.122, bf16[24,768]{1,0:T(8,128)(2,1)S(1)} %convert_element_type.191, bf16[768,768]{1,0:T(8,128)(2,1)S(1)} %bitcast.121), kind=kOutput, calls=%fused_computation.31 | convolution fusion | flops 56807424 | bytes 2433024 | tf_op jit(solution)/shard_map/dot_general | solution.py:224
  180.3 5.7 %exchange6.1 = bf16[4,24,768]{2,1,0:T(8,128)(2,1)} custom-call(bf16[24,768]{1,0:T(8,128)(2,1)} %convolution_convert_fusion.7.refs_0_), custom_call_target="tpu_custom_call" | custom-call | tf_op jit(solution)/shard_map/exchange6/pallas_call | solution.py:198
  186.0 0.9 convert_reduce_fusion.3
  187.5 0.8 fusion.16.refs_0_
  188.4 8.1 %exchange7.1 = bf16[8,8,768]{2,1,0:T(8,128)(2,1)} custom-call(bf16[8,8,768]{2,1,0:T(8,128)(2,1)} %fusion.16.refs_0_), custom_call_target="tpu_custom_call" | custom-call | tf_op jit(solution)/shard_map/exchange7/pallas_call | solution.py:198
  196.5 1.0 reshape.373
  202.7 8.1 %exchange8.1 = bf16[8,8,768]{2,1,0:T(8,128)(2,1)} custom-call(bf16[8,8,768]{2,1,0:T(8,128)(2,1)} %reshape.376.refs_0_), custom_call_target="tpu_custom_call" | custom-call | tf_op jit(solution)/shard_map/exchange8/pallas_call | solution.py:198
  210.8 1.0 convolution_convert_fusion.14
  212.4 1.0 fusion.117
  213.4 0.9 fusion.79
  214.3 1.3 fusion.69
  215.6 1.6 fusion.114
  217.2 1.6 fusion.116
  (138 shorter events, 19.2 us)
Async XLA Ops:
  0.6 197.0 %copy-start = (bf16[4,768,256]{2,1,0:T(8,128)(2,1)S(1)}, bf16[4,768,256]{2,1,0:T(8,128)(2,1)}, u32[]{:S(2)}) copy-start(bf16[4,768,256]{2,1,0:T(8,128)(2,1)} %param.30) | copy-start | bytes 4718596
  0.6 11.3 %copy-start.1 = (bf16[192,768]{1,0:T(8,128)(2,1)S(1)}, bf16[192,768]{1,0:T(8,128)(2,1)}, u32[]{:S(2)}) copy-start(bf16[192,768]{1,0:T(8,128)(2,1)} %param.18) | copy-start | bytes 884740
  0.7 10.4 %copy-start.17 = (bf16[12,2,56]{2,1,0:T(2,128)(2,1)S(1)}, bf16[12,2,56]{2,1,0:T(2,128)(2,1)}, u32[]{:S(2)}) copy-start(bf16[12,2,56]{2,1,0:T(2,128)(2,1)} %param.28) | copy-start | bytes 8068
  0.7 12.2 %copy-start.8 = (bf16[2,3,96,192]{3,2,1,0:T(8,128)(2,1)S(1)}, bf16[2,3,96,192]{3,2,1,0:T(8,128)(2,1)}, u32[]{:S(2)}) copy-start(bf16[2,3,96,192]{3,2,1,0:T(8,128)(2,1)} %param.21) | copy-start | bytes 663556
  10.7 3.0 %copy-start.9 = (bf16[2,96,768]{2,1,0:T(8,128)(2,1)S(1)}, bf16[2,96,768]{2,1,0:T(8,128)(2,1)}, u32[]{:S(2)}) copy-start(bf16[2,96,768]{2,1,0:T(8,128)(2,1)} %param.23) | copy-start | bytes 884740
  11.1 3.3 %copy-start.14 = (bf16[64,24]{0,1:T(8,128)(2,1)}, bf16[64,24]{0,1:T(8,128)(2,1)S(1)}, u32[]{:S(2)}) copy-start(bf16[64,24]{0,1:T(8,128)(2,1)S(1)} %reshape.347) | copy-start | bytes 9220
  11.9 2.5 %copy-start.10 = (bf16[2,768,96]{1,2,0:T(8,128)(2,1)S(1)}, bf16[2,768,96]{1,2,0:T(8,128)(2,1)}, u32[]{:S(2)}) copy-start(bf16[2,768,96]{1,2,0:T(8,128)(2,1)} %param.24) | copy-start | bytes 884740
  42.8 1.6 copy-start.23
  42.8 1.7 copy-start.12
  45.5 0.6 copy-start.6
  47.4 2.7 %copy-start.7 = (pred[12,64,64]{1,2,0:T(8,128)(4,1)S(1)}, pred[12,64,64]{1,2,0:T(8,128)(4,1)}, u32[]{:S(2)}) copy-start(pred[12,64,64]{1,2,0:T(8,128)(4,1)} %copy-done.6) | copy-start | bytes 147460
  81.6 0.7 copy-start.20
  128.9 1.0 copy-start.19
  129.1 32.9 %copy-start.5 = (bf16[8,96,768]{2,1,0:T(8,128)(2,1)S(1)}, bf16[8,96,768]{2,1,0:T(8,128)(2,1)}, u32[]{:S(2)}) copy-start(bf16[8,96,768]{2,1,0:T(8,128)(2,1)} %get-tuple-element.32) | copy-start | bytes 3538948
  164.4 0.7 copy-start.24
  166.7 10.5 %copy-start.13 = (f32[4,3,2,768]{3,2,1,0:T(2,128)S(1)}, f32[4,3,2,768]{3,2,1,0:T(2,128)}, u32[]{:S(2)}) copy-start(f32[4,3,2,768]{3,2,1,0:T(2,128)} %get-tuple-element.30) | copy-start | bytes 221188
  166.7 10.8 %copy-start.22 = (f32[768]{0:T(1024)S(1)}, f32[768]{0:T(1024)}, u32[]{:S(2)}) copy-start(f32[768]{0:T(1024)} %get-tuple-element.60) | copy-start | bytes 9220
  166.7 11.0 %copy-start.4 = (bf16[8,96,768]{2,1,0:T(8,128)(2,1)S(1)}, bf16[8,96,768]{2,1,0:T(8,128)(2,1)}, u32[]{:S(2)}) copy-start(bf16[8,96,768]{2,1,0:T(8,128)(2,1)} %get-tuple-element.33) | copy-start | bytes 3538948
  177.7 9.6 %copy-start.21 = (f32[768]{0:T(1024)S(1)}, f32[768]{0:T(1024)}, u32[]{:S(2)}) copy-start(f32[768]{0:T(1024)} %get-tuple-element.56) | copy-start | bytes 9220
  177.7 9.8 %copy-start.15 = (bf16[64,24]{0,1:T(8,128)(2,1)S(1)}, bf16[64,24]{0,1:T(8,128)(2,1)}, u32[]{:S(2)}) copy-start(bf16[64,24]{0,1:T(8,128)(2,1)} %copy-done.14) | copy-start | bytes 9220
  196.5 1.5 copy-start.11
  196.5 1.5 copy-start.16
  196.5 1.5 copy-start.18
  197.5 1.0 copy-start.2
  197.7 1.1 copy-start.3
  198.0 0.9 copy-start.25
  198.0 0.9 copy-start.26
  198.0 1.0 copy-start.27
where the time goes:
time: 220 us; the launch traced here: 219 us
  Pallas kernels  141 us (64%)
  matrix products  37.9 us (17%)
  local copies, waits for them, and re-layouts  20.5 us (9%)
  other arithmetic  18.2 us (8%)
    pallas_call x9, Pallas kernels, exchange(): pl.pallas_call(functools.partial(exchange_kernel, n_dp, n_mp, kinds), out...  141 us
    dot_general x4, matrix products, dot_turned(): lax.dot_general(left, right, (((1,), (1,)), ((), ())), preferred_element_...  12.5 us
    dot_general x5, matrix products, dot32(): return jnp.dot(left, right, preferred_element_type=jnp.float32)  6.39 us
    reduce_sum x4, other arithmetic, added(): return jnp.sum(blocks.astype(jnp.float32), axis=0)  4.86 us
    dot_general x2, matrix products, attend(): jnp.einsum('shqk,skhd->sqhd', shares, value_rows, preferred_element_type=...  4.65 us

commit v1 on v0

--- a/solution.py
+++ b/solution.py
@@ -253,37 +253,563 @@
     return pullback(jnp.ones((), jnp.float32))
 
 
-def on_device(
+CHUNK = 64
+
+
+def remote(source, landing, send_sem, recv_sem, where):
+    return pltpu.make_async_remote_copy(
+        src_ref=source,
+        dst_ref=landing,
+        send_sem=send_sem,
+        recv_sem=recv_sem,
+        device_id=where,
+        device_id_type=MESH_ID,
+    )
+
+
+def trunk_kernel(
+    n_dp,
+    n_mp,
     tokens,
     obs_mask,
     norm_gains,
-    attn_in,
-    attn_out,
-    mlp_in,
-    mlp_out,
-    embodiment,
-    levels,
-    actions,
-    noise,
-    action_dims,
-    head_read,
-    head_act,
-    time_table,
-    block_in,
-    block_out,
-    head_out,
+    joined,
+    raising,
+    lowering,
+    ends_out,
+    full,
+    cast_rows,
+    residual,
+    projected,
+    context,
+    hidden,
+    partial_rows,
+    near_part,
+    far_part,
+    own_part,
+    paired,
+    mask_all,
+    ends_all,
+    end_terms,
+    out_weight,
+    z_send,
+    z_recv,
+    y_send,
+    y_recv,
+    keep_sem,
+    cast_send,
+    cast_recv,
+    sum_send,
+    sum_recv,
+    ends_send,
+    ends_recv,
+    term_send,
+    term_recv,
+    mask_send,
+    mask_recv,
 ):
+    layer_count = joined.shape[0]
+    rows, model = residual.shape
+    block = joined.shape[1]
+    samples, length = obs_mask.shape
+    width = model // n_mp
+    wide = model // 3
+    pad = wide - width
+    heads = width // HDIM
+    columns = n_dp // 2
+    chunks = rows // CHUNK
+    f32, bf16 = jnp.float32, jnp.bfloat16
+
+    my_dp, my_mp = lax.axis_index("dp"), lax.axis_index("mp")
+    my_z, my_y = my_dp // 2, my_dp % 2
+    y_peer = {"dp": my_z * 2 + 1 - my_y}
+    core = my_mp % 2
+    sib = my_mp + 1 - 2 * core
+    far = (my_mp + 2) % n_mp
+    far_sib = (sib + 2) % n_mp
+    sib_id, far_id = {"mp": sib}, {"mp": far}
+
+    barrier = pltpu.get_barrier_semaphore()
+    for offset in range(1, n_mp):
+        pl.semaphore_signal(
+            barrier, inc=1, device_id={"mp": (my_mp + offset) % n_mp}, device_id_type=MESH_ID
+        )
+    for offset in range(1, columns):
+        pl.semaphore_signal(
+            barrier,
+            inc=1,
+            device_id={"dp": ((my_z + offset) % columns) * 2 + my_y},
+            device_id_type=MESH_ID,
+        )
+    pl.semaphore_signal(barrier, inc=1, device_id=y_peer, device_id_type=MESH_ID)
+
+    def gain(index):
+        return norm_gains[index : index + 1, :]
+
+    def norm_chunk(index, chunk, gain_index):
+        at = pl.ds(chunk * CHUNK, CHUNK)
+        cast_rows[index, my_mp, at, :] = normalize(residual[at, :], gain(gain_index)).astype(bf16)
+
+    for chunk in range(chunks):
+        at = pl.ds(chunk * CHUNK, CHUNK)
+        residual[at, :] = tokens[at, :].astype(f32)
+        norm_chunk(0, chunk, 0)
+    mask_all[my_mp] = obs_mask[...]
+    pl.semaphore_wait(barrier, n_mp - 1 + columns)
+
+    sources = [part.at[layer] for layer in range(layer_count) for part in (joined, raising, lowering)]
+
+    def spot(unit, origin):
+        return full.at[unit, pl.ds(pl.multiple_of(origin * block, block), block)]
+
+    def z_copy(unit, offset):
+        return remote(
+            sources[unit],
+            spot(unit, my_dp),
+            z_send.at[unit, offset],
+            z_recv.at[unit, offset],
+            {"dp": ((my_z + offset) % columns) * 2 + my_y},
+        )
+
+    def z_landed(unit, offset):
+        origin = ((my_z + columns - offset) % columns) * 2 + my_y
+        return remote(
+            sources[unit],
+            spot(unit, origin),
+            z_send.at[unit, offset],
+            z_recv.at[unit, offset],
+            {"dp": origin},
+        )
+
+    def y_copy(unit, offset):
+        origin = ((my_z + columns - offset) % columns) * 2 + my_y
+        return remote(
+            sources[unit] if offset == 0 else spot(unit, origin),
+            spot(unit, origin),
+            y_send.at[unit, offset],
+            y_recv.at[unit, offset],
+            y_peer,
+        )
+
+    def y_landed(unit, offset):
+        origin = ((my_z + columns - offset) % columns) * 2 + 1 - my_y
+        return remote(
+            sources[unit],
+            spot(unit, origin),
+            y_send.at[unit, offset],
+            y_recv.at[unit, offset],
+            y_peer,
+        )
+
+    def kept(unit):
+        return pltpu.make_async_copy(sources[unit], spot(unit, my_dp), keep_sem.at[unit])
+
+    def z_start(unit):
+        for offset in range(1, columns):
+            z_copy(unit, offset).start()
+        kept(unit).start()
+
+    def relay(unit, offset):
+        z_landed(unit, offset).wait_recv()
+        y_copy(unit, offset).start()
+
+    def relay_all(unit):
+        for offset in range(1, columns):
+            relay(unit, offset)
+
+    def complete(unit):
+        for offset in range(columns):
+            y_landed(unit, offset).wait_recv()
+        kept(unit).wait()
+
+    def cast_copy(index, way, chunk):
+        at = pl.ds(chunk * CHUNK, CHUNK)
+        whose = far if way == 2 else my_mp
+        place = cast_rows.at[index, whose, at]
+        return remote(
+            place,
+            place,
+            cast_send.at[index, way, chunk],
+            cast_recv.at[index, way, chunk],
+            far_id if way == 1 else sib_id,
+        )
+
+    def cast_landed(index, way, chunk):
+        at = pl.ds(chunk * CHUNK, CHUNK)
+        place = cast_rows.at[index, (sib, far, far_sib)[way], at]
+        return remote(
+            place,
+            place,
+            cast_send.at[index, way, chunk],
+            cast_recv.at[index, way, chunk],
+            far_id if way == 1 else sib_id,
+        )
+
+    def cast_pass(index, chunk):
+        cast_landed(index, 1, chunk).wait_recv()
+        cast_copy(index, 2, chunk).start()
+
+    def cast_near(index):
+        for chunk in range(chunks):
+            cast_landed(index, 0, chunk).wait_recv()
+
+    def cast_far(index):
+        for chunk in range(chunks):
+            cast_landed(index, 2, chunk).wait_recv()
+
+    def sum_near(index):
+        return remote(
+            partial_rows.at[far_sib],
+            near_part.at[index],
+            sum_send.at[index, 0, 0],
+            sum_recv.at[index, 0, 0],
+            sib_id,
+        )
+
+    def sum_own(index):
+        return remote(
+            partial_rows.at[sib],
+            own_part.at[index],
+            sum_send.at[index, 1, 0],
+            sum_recv.at[index, 1, 0],
+            sib_id,
+        )
+
+    def sum_far(index, chunk):
+        at = pl.ds(chunk * CHUNK, CHUNK)
+        return remote(
+            paired.at[index, at],
+            far_part.at[index, at],
+            sum_send.at[index, 2, chunk],
+            sum_recv.at[index, 2, chunk],
+            far_id,
+        )
+
+    def sum_cross(index):
+        sum_near(index).wait_recv()
+        for chunk in range(chunks):
+            at = pl.ds(chunk * CHUNK, CHUNK)
+            paired[index, at, :] = (
+                partial_rows[far, at, :].astype(f32) + near_part[index, at, :].astype(f32)
+            ).astype(bf16)
+            sum_far(index, chunk).start()
+
+    def sum_finish(index, next_cast, gain_index):
+        sum_own(index).wait_recv()
+        for chunk in range(chunks):
+            at = pl.ds(chunk * CHUNK, CHUNK)
+            sum_far(index, chunk).wait_recv()
+            residual[at, :] = (
+                residual[at, :]
+                + own_part[index, at, :].astype(f32)
+                + far_part[index, at, :].astype(f32)
+            )
+            norm_chunk(next_cast, chunk, gain_index)
+            cast_copy(next_cast, 1, chunk).start()
+            cast_copy(next_cast, 0, chunk).start()
+
+    def peers():
+        return [(offset, {"mp": (my_mp + offset) % n_mp}) for offset in range(1, n_mp)]
+
+    def ends_copy(offset, who):
+        return remote(
+            ends_all.at[my_mp], ends_all.at[my_mp], ends_send.at[offset], ends_recv.at[offset], who
+        )
+
+    def term_copy(index, offset, who):
+        place = end_terms.at[index, my_mp]
+        return remote(place, place, term_send.at[index, offset], term_recv.at[index, offset], who)
+
+    def term_landed(index, offset):
+        place = end_terms.at[index, (my_mp + n_mp - offset) % n_mp]
+        return remote(
+            place, place, term_send.at[index, offset], term_recv.at[index, offset], sib_id
+        )
+
+    def mask_copy(offset, who):
+        return remote(
+            obs_mask, mask_all.at[my_mp], mask_send.at[offset], mask_recv.at[offset], who
+        )
+
+    z_start(0)
+    y_copy(0, 0).start()
+    for offset, who in peers():
+        mask_copy(offset, who).start()
+    for chunk in range(chunks):
+        cast_copy(0, 1, chunk).start()
+        cast_copy(0, 0, chunk).start()
+    z_start(1)
+    for step in range(max(chunks, columns - 1)):
+        if step < chunks:
+            cast_pass(0, step)
+        if step < columns - 1:
+            relay(0, step + 1)
+    y_copy(1, 0).start()
+    z_start(2)
+
+    lane = lax.broadcasted_iota(jnp.int32, (1, wide), 1)
+    lane_masks = [
+        jnp.where((lane >= head * HDIM) & (lane < (head + 1) * HDIM), 1.0, 0.0).astype(f32)
+        for head in range(heads)
+    ]
+
+    def take_out_weight(unit):
+        row = lax.broadcasted_iota(jnp.int32, (model, wide), 0)
+        spot_lane = lax.broadcasted_iota(jnp.int32, (model, wide), 1)
+        picks = (row % wide >= width) & (spot_lane == (row // wide) * pad + row % wide - width)
+        choose = jnp.where(picks, 1.0, 0.0).astype(bf16)
+        out_weight[...] = dot32(full[unit], choose).astype(bf16)
+
+    def pair_rows(first, body):
+        def step(index, carry):
+            body(first + index)
+            return carry
+
+        lax.fori_loop(0, 2, step, 0)
+
+    near_first = my_mp - core
+    far_first = (near_first + 2) % n_mp
+
+    def project(index, unit, owner):
+        at = pl.ds(pl.multiple_of(owner * rows, rows), rows)
+        projected[at, :] = dot32(cast_rows[index, owner], full[unit]).astype(bf16)
+
+    def attention(tail_rows):
+        asked = tail_rows if tail_rows else length
+        row = lax.broadcasted_iota(jnp.int32, (heads * asked, length), 0) % asked
+        col = lax.broadcasted_iota(jnp.int32, (heads * asked, length), 1)
+        itself = jnp.where(row + (length - asked) == col, 1.0, 0.0)
+        narrow = lax.broadcasted_iota(jnp.int32, (1, length), 1)
+
+        def step(owner, carry):
+            for sample in range(samples):
+                start = owner * rows + sample * length
+                at = pl.ds(pl.multiple_of(start, length), length)
+                ask = pl.ds(pl.multiple_of(start + length - asked, 16), asked)
+                query = projected[ask, :wide].astype(f32) * HDIM ** (-0.5)
+                stacked = jnp.concatenate(
+                    [(query * lanes).astype(bf16) for lanes in lane_masks], axis=0
+                )
+                scores = dot_turned(stacked, projected[at, wide : 2 * wide])
+                seen = mask_all[owner, sample : sample + 1, :]
+                seen = jnp.where((seen == 1) & (narrow < length - READ), 1.0, 0.0)
+                weights = jnp.where(jnp.maximum(itself, seen) > 0.0, jnp.exp(scores), 0.0)
+                shares = (weights / jnp.sum(weights, axis=-1, keepdims=True)).astype(bf16)
+                mixed = dot32(shares, projected[at, 2 * wide :])
+                total = mixed[:asked] * lane_masks[0]
+                for head in range(1, heads):
+                    total = total + mixed[head * asked : (head + 1) * asked] * lane_masks[head]
+                put = pl.ds(
+                    pl.multiple_of(owner * (samples * asked) + sample * asked, 16), asked
+                )
+                context[put, :] = total.astype(bf16)
+            return carry
+
+        lax.fori_loop(0, n_mp, step, 0)
+
+    def combine(index, part_of, late):
+        if index:
+            sum_near(index - 1).wait_send()
+            sum_own(index - 1).wait_send()
+        partial_rows[far_sib] = part_of(far_sib).astype(bf16)
+        sum_near(index).start()
+        partial_rows[far] = part_of(far).astype(bf16)
+        partial_rows[sib] = part_of(sib).astype(bf16)
+        sum_own(index).start()
+        sum_cross(index)
+        residual[...] = residual[...] + part_of(my_mp)
+        late()
+
+    complete(0)
+    cast_near(0)
+    cast_far(0)
+    for offset, who in peers():
+        mask_copy(offset, who).wait_recv()
+    take_out_weight(0)
+    pair_rows(near_first, lambda owner: project(0, 0, owner))
+    pair_rows(far_first, lambda owner: project(0, 0, owner))
+    attention(0)
+
+    def attended(owner):
+        at = pl.ds(pl.multiple_of(owner * rows, rows), rows)
+        return dot_turned(context[at, :], out_weight[...])
+
+    def after_attention():
+        relay_all(1)
+        y_copy(2, 0).start()
+        z_start(3)
+
+    combine(0, attended, after_attention)
+    sum_finish(0, 1, 1)
+    for chunk in range(chunks):
+        cast_pass(1, chunk)
+    complete(1)
+
+    def raise_rows(owner):
+        hidden[owner] = jax.nn.gelu(dot32(cast_rows[1, owner], full[1]), approximate=True).astype(
+            bf16
+        )
+
+    cast_near(1)
+    pair_rows(near_first, raise_rows)
+    relay_all(2)
+    y_copy(3, 0).start()
+    z_start(4)
+    cast_far(1)
+    pair_rows(far_first, raise_rows)
+    complete(2)
+
+    def lowered_rows(owner):
+        return dot_turned(hidden[owner], full[2])
+
+    def after_mlp():
+        relay_all(3)
+        y_copy(4, 0).start()
+        z_start(5)
+
+    combine(1, lowered_rows, after_mlp)
+    sum_finish(1, 2, 2)
+    ends_all[my_mp] = jnp.zeros(ends_all.shape[1:], f32)
+    for sample in range(samples):
+        last = (sample + 1) * length
+        ends_all[my_mp, READ * sample : READ * (sample + 1), :] = residual[last - READ : last, :]
+    for offset, who in peers():
+        ends_copy(offset, who).start()
+    for chunk in range(chunks):
+        cast_pass(2, chunk)
+    complete(3)
+    take_out_weight(3)
+    cast_near(2)
+    pair_rows(near_first, lambda owner: project(2, 3, owner))
+    relay_all(4)
+    y_copy(5, 0).start()
+    cast_far(2)
+    pair_rows(far_first, lambda owner: project(2, 3, owner))
+    attention(16)
+
+    slots = ends_all.shape[1]
+    row = lax.broadcasted_iota(jnp.int32, (n_mp * slots, n_mp * samples * 16), 0)
+    col = lax.broadcasted_iota(jnp.int32, (n_mp * slots, n_mp * samples * 16), 1)
+    inner = row % slots
+    wanted = ((row // slots) * samples + inner // READ) * 16 + 16 - READ + inner % READ
+    choose = jnp.where((wanted == col) & (inner < samples * READ), 1.0, 0.0).astype(bf16)
+    ends_context = dot32(choose, context[: n_mp * samples * 16, :]).astype(bf16)
+
+    def share(index, value):
+        end_terms[index, my_mp] = value.astype(bf16)
+        for offset, who in peers():
+            term_copy(index, offset, who).start()
+
+    def gathered_terms(index, ends):
+        for offset in range(1, n_mp):
+            term_landed(index, offset).wait_recv()
+        for owner in range(n_mp):
+            ends = ends + end_terms[index, owner].astype(f32)
+        return ends
+
+    share(0, dot_turned(ends_context, out_weight[...]))
+    for offset, who in peers():
+        remote(
+            ends_all.at[my_mp],
+            ends_all.at[(my_mp + n_mp - offset) % n_mp],
+            ends_send.at[offset],
+            ends_recv.at[offset],
+            who,
+        ).wait_recv()
+    relay_all(5)
+    ends = jnp.concatenate([ends_all[owner] for owner in range(n_mp)], axis=0)
+    ends = gathered_terms(0, ends)
+    normed = normalize(ends, gain(3)).astype(bf16)
+    complete(4)
+    raised = jax.nn.gelu(dot32(normed, full[4]), approximate=True).astype(bf16)
+    complete(5)
+    share(1, dot_turned(raised, full[5]))
+    ends = gathered_terms(1, ends)
+    ends_out[...] = normalize(ends, gain(4)).astype(bf16)
+
+    for unit in range(len(sources)):
+        for offset in range(columns):
+            if offset:
+                z_copy(unit, offset).wait_send()
+            y_copy(unit, offset).wait_send()
+    for index in range(3):
+        for way in range(3):
+            for chunk in range(chunks):
+                cast_copy(index, way, chunk).wait_send()
+    for index in range(2):
+        if index == 1:
+            sum_near(index).wait_send()
+            sum_own(index).wait_send()
+        for chunk in range(chunks):
+            sum_far(index, chunk).wait_send()
+    for offset, who in peers():
+        mask_copy(offset, who).wait_send()
+        ends_copy(offset, who).wait_send()
+        for index in range(2):
+            term_copy(index, offset, who).wait_send()
+
+
+def trunk(tokens, obs_mask, norm_gains, joined, raising, lowering):
+    n_dp, n_mp = lax.axis_size("dp"), lax.axis_size("mp")
+    rows, model = tokens.shape
+    samples = obs_mask.shape[0]
+    wide = model // 3
+    units = 3 * joined.shape[0]
+    columns, chunks = n_dp // 2, rows // CHUNK
+    slots = samples * READ + (-samples * READ) % 8
+    bf16, f32 = jnp.bfloat16, jnp.float32
+    dma = pltpu.SemaphoreType.DMA
+    vmem = pltpu.VMEM
+    return pl.pallas_call(
+        functools.partial(trunk_kernel, n_dp, n_mp),
+        out_shape=jax.ShapeDtypeStruct((n_mp * slots, model), bf16),
+        in_specs=[pl.BlockSpec(memory_space=vmem)] * 6,
+        out_specs=pl.BlockSpec(memory_space=vmem),
+        scratch_shapes=[
+            vmem((units, model, model), bf16),
+            vmem((3, n_mp, rows, model), bf16),
+            vmem((rows, model), f32),
+            vmem((n_mp * rows, model), bf16),
+            vmem((n_mp * rows, wide), bf16),
+            vmem((n_mp, rows, model), bf16),
+            vmem((n_mp, rows, model), bf16),
+            vmem((2, rows, model), bf16),
+            vmem((2, rows, model), bf16),
+            vmem((2, rows, model), bf16),
+            vmem((2, rows, model), bf16),
+            vmem((n_mp,) + obs_mask.shape, jnp.int32),
+            vmem((n_mp, slots, model), f32),
+            vmem((2, n_mp, n_mp * slots, model), bf16),
+            vmem((model, wide), bf16),
+            dma((units, columns)),
+            dma((units, columns)),
+            dma((units, columns)),
+            dma((units, columns)),
+            dma((units,)),
+            dma((3, 3, chunks)),
+            dma((3, 3, chunks)),
+            dma((2, 3, chunks)),
+            dma((2, 3, chunks)),
+            dma((n_mp,)),
+            dma((n_mp,)),
+            dma((2, n_mp)),
+            dma((2, n_mp)),
+            dma((n_mp,)),
+            dma((n_mp,)),
+        ],
+        compiler_params=pltpu.CompilerParams(collective_id=50, has_side_effects=True),
+        name="trunk",
+    )(tokens, obs_mask, norm_gains, joined, raising, lowering)
+
+
+def general_trunk(ident, tokens, obs_mask, norm_gains, attn_in, attn_out, mlp_in, mlp_out, small):
     model = tokens.shape[1]
-    act = actions.shape[2]
     width = attn_in.shape[3]
     heads_local = width // HDIM
     samples_local, length = obs_mask.shape
     layer_count = attn_in.shape[0]
-    n_mp, n_dp = lax.axis_size("mp"), lax.axis_size("dp")
-    my_model, my_owner = lax.axis_index("mp"), lax.axis_index("dp")
+    n_mp = lax.axis_size("mp")
     samples_group = samples_local * n_mp
-    ident = iter(range(100))
-
     joined = [
         jnp.concatenate(
             [attn_in[layer, 0], attn_in[layer, 1], attn_in[layer, 2], attn_out[layer].T], axis=1
@@ -292,25 +818,6 @@
     ]
     lowered = [mlp_out[layer].T for layer in range(layer_count)]
 
-    heads_dev = head_read.shape[0]
-    slot_count = heads_dev * n_dp
-    owners = embodiment[:, 0]
-    table = plan()
-    onto = (jnp.arange(slot_count)[:, None] == owners[None, :]).astype(jnp.bfloat16)
-    spread_rows = jnp.einsum("es,rq->ersq", onto, jnp.eye(READ, dtype=jnp.bfloat16)).reshape(
-        slot_count * READ, samples_group * READ
-    )
-    small = jnp.concatenate(
-        [
-            noisy_pair(levels, actions, noise, table),
-            noise,
-            (levels + 1)[..., None].astype(jnp.bfloat16),
-        ],
-        axis=-1,
-    ).reshape(samples_group * READ, 2 * act + 1)
-    small = jnp.pad(small, ((0, 0), (0, -small.shape[1] % 128)))
-    small = dot32(spread_rows, small).astype(jnp.bfloat16)
-    small = small.reshape(n_dp, heads_dev * READ, small.shape[1])
 
     residual = tokens.astype(jnp.float32)
     wide = None
@@ -385,11 +892,100 @@
         wide = wide.reshape(model, -1)
         residual = residual + added(terms)
 
-    readouts = normalize(ends, norm_gains[2 * layer_count]).astype(jnp.bfloat16)
+    return normalize(ends, norm_gains[2 * layer_count]).astype(jnp.bfloat16), got_small
+
+
+def fused_trunk(ident, tokens, obs_mask, norm_gains, attn_in, attn_out, mlp_in, mlp_out, small):
+    model = tokens.shape[1]
+    width = attn_in.shape[3]
+    pad = model // 3 - width
+    samples_local = obs_mask.shape[0]
+    n_mp = lax.axis_size("mp")
+    pieces = []
+    turned = jnp.swapaxes(attn_out, 1, 2)
+    for part in range(3):
+        pieces += [attn_in[:, part], turned[:, :, part * pad : (part + 1) * pad]]
+    joined = jnp.concatenate(pieces, axis=2)
+    ends = trunk(tokens, obs_mask, norm_gains, joined, mlp_in, jnp.swapaxes(mlp_out, 1, 2))
+    ends = ends.reshape(n_mp, -1, model)[:, : samples_local * READ]
+    return ends.reshape(-1, model), None
+
+
+def fits_fused(tokens, obs_mask, attn_in, mlp_in):
+    n_mp, n_dp = lax.axis_size("mp"), lax.axis_size("dp")
+    model, width = tokens.shape[1], attn_in.shape[3]
+    pad = model // 3 - width
+    return (
+        n_mp == 4
+        and n_dp % 2 == 0
+        and attn_in.shape[0] == 2
+        and attn_in.shape[2] % 16 == 0
+        and mlp_in.shape[2] == model
+        and (model // 3) % 128 == 0
+        and 3 * pad == width
+        and tokens.shape[0] % CHUNK == 0
+        and obs_mask.shape[1] == CHUNK
+    )
+
+
+def on_device(
+    tokens,
+    obs_mask,
+    norm_gains,
+    attn_in,
+    attn_out,
+    mlp_in,
+    mlp_out,
+    embodiment,
+    levels,
+    actions,
+    noise,
+    action_dims,
+    head_read,
+    head_act,
+    time_table,
+    block_in,
+    block_out,
+    head_out,
+):
+    model = tokens.shape[1]
+    act = actions.shape[2]
+    samples_local = obs_mask.shape[0]
+    n_mp, n_dp = lax.axis_size("mp"), lax.axis_size("dp")
+    my_model, my_owner = lax.axis_index("mp"), lax.axis_index("dp")
+    samples_group = samples_local * n_mp
+    ident = iter(range(100))
+
+    heads_dev = head_read.shape[0]
+    slot_count = heads_dev * n_dp
+    owners = embodiment[:, 0]
+    table = plan()
+    onto = (jnp.arange(slot_count)[:, None] == owners[None, :]).astype(jnp.bfloat16)
+    spread_rows = jnp.einsum("es,rq->ersq", onto, jnp.eye(READ, dtype=jnp.bfloat16)).reshape(
+        slot_count * READ, samples_group * READ
+    )
+    small = jnp.concatenate(
+        [
+            noisy_pair(levels, actions, noise, table),
+            noise,
+            (levels + 1)[..., None].astype(jnp.bfloat16),
+        ],
+        axis=-1,
+    ).reshape(samples_group * READ, 2 * act + 1)
+    small = jnp.pad(small, ((0, 0), (0, -small.shape[1] % 128)))
+    small = dot32(spread_rows, small).astype(jnp.bfloat16)
+    small = small.reshape(n_dp, heads_dev * READ, small.shape[1])
+
+    run = fused_trunk if fits_fused(tokens, obs_mask, attn_in, mlp_in) else general_trunk
+    readouts, got_small = run(
+        ident, tokens, obs_mask, norm_gains, attn_in, attn_out, mlp_in, mlp_out, small
+    )
     send = dot32(spread_rows, readouts).astype(jnp.bfloat16)
-    (got_features,) = exchange(
-        next(ident), ("swap", send.reshape(n_dp, heads_dev * READ, model))
-    )
+    send = send.reshape(n_dp, heads_dev * READ, model)
+    if got_small is None:
+        got_features, got_small = exchange(next(ident), ("swap", send), ("swap", small))
+    else:
+        (got_features,) = exchange(next(ident), ("swap", send))
 
     def by_head(values):
         values = values.reshape(n_dp, heads_dev, READ, values.shape[-1])

time: 220 us -> 155 us (0.70)
  matrix products: 37.9 us -> 12.3 us
  other arithmetic: 18.2 us -> 1.94 us
  local copies, waits for them, and re-layouts: 20.5 us -> 7.58 us
  Pallas kernels: 141 us -> 132 us
    pallas_call x9 -> x2, Pallas kernels: 141 us -> 22.8 us  [exchange(): pl.pallas_call(functools.partial(exchange_kernel, n_dp, n_mp, kinds), out...]
    pallas_call x0 -> x1, Pallas kernels: none -> 109 us  [trunk(): pl.pallas_call(functools.partial(trunk_kernel, n_dp, n_mp), out_shape=jax...]
    dot_general x8 -> x0, matrix products: 20.3 us -> none  [the longest x4 12.5 us: dot_turned(): lax.dot_general(left, right, (((1,), (1,)), ((), ())), preferred_element_...]
    reduce_sum x14 -> x0, other arithmetic: 8.51 us -> none  [the longest x4 4.86 us: added(): return jnp.sum(blocks.astype(jnp.float32), axis=0)]
    slice x8 -> x1, local copies, waits for them, and re-layouts: 5.06 us -> 0.09 us  [fused_trunk(): pieces += [attn_in[:, part], turned[:, :, part * pad:(part + 1) * pad]]]
    reshape x9 -> x1, local copies, waits for them, and re-layouts: 5.64 us -> 0.85 us  [fused_trunk(): return (ends.reshape(-1, model), None)]
    dot_general x5 -> x2, matrix products: 6.39 us -> 1.66 us  [dot32(): return jnp.dot(left, right, preferred_element_type=jnp.float32)]
    convert_element_type x5 -> x0, other arithmetic: 2.87 us -> none  [the longest x2 1.78 us: on_device(): normed = normalize(residual, norm_gains[2 * layer]).astype(jnp.bfloat16)]
where the time goes in v1:
time: 155 us
  Pallas kernels  132 us (85%)
  matrix products  12.3 us (8%)
  local copies, waits for them, and re-layouts  7.58 us (5%)
  other arithmetic  1.94 us (1%)
    pallas_call x1, Pallas kernels, trunk(): pl.pallas_call(functools.partial(trunk_kernel, n_dp, n_mp), out_shape=jax...  109 us
    pallas_call x2, Pallas kernels, exchange(): pl.pallas_call(functools.partial(exchange_kernel, n_dp, n_mp, kinds), out...  22.8 us

profile of v1, /device:TPU:0, one launch (start us, length us, event | category | flops | bytes accessed | tf_op | source)
XLA Modules:
  0.0 154.6 jit_solution(10214949362751814468)
XLA Ops:
  0.6 0.0 copy-start
  0.6 0.8 fusion.33
  1.5 0.1 multiply_bitcast_fusion
  1.6 0.2 reshape.126
  1.9 1.0 slice_bitcast_fusion
  2.9 1.0 copy.50
  3.9 0.1 fusion.54
  4.0 0.9 concatenate.13.joined
  4.9 109.1 %trunk.1 = bf16[32,768]{1,0:T(8,128)(2,1)} custom-call(bf16[192,768]{1,0:T(8,128)(2,1)} %tokens.1, s32[3,64]{1,0:T(4,128)} %obs_mask.1, f32[5,768]{1,0:T(8,128)} %norm_gains.1, bf16[2,96,768]{2,1,0:T(8,128)(2,1)} %concatenate.13.joined, bf16[2,96,768]{2,1,0:T(8,128)(2,1)} %raising.1, bf16[2,96,768]{2,1,0:T(8,128)(2,1)} %bitcast.71), custom_call_target="tpu_custom_call" | custom-call | tf_op jit(solution)/shard_map/trunk/pallas_call | solution.py:763
  114.0 0.8 reshape.128
  114.8 0.8 fusion.refs_0_
  115.7 0.1 copy.54
  115.8 0.1 concatenate.18
  115.9 0.1 multiply_multiply_fusion.2
  116.0 0.1 copy.53
  116.1 0.2 fusion.29
  116.3 0.1 add_convert_fusion
  116.4 0.8 fusion.5.refs_1_
  117.2 14.7 %exchange0.1 = (bf16[8,8,768]{2,1,0:T(8,128)(2,1)}, bf16[8,8,128]{2,1,0:T(8,128)(2,1)}) custom-call(bf16[8,8,768]{2,1,0:T(8,128)(2,1)} %fusion.refs_0_, bf16[8,8,128]{2,1,0:T(8,128)(2,1)} %fusion.5.refs_1_), custom_call_target="tpu_custom_call" | custom-call | tf_op jit(solution)/shard_map/exchange0/pallas_call | solution.py:198
  131.8 0.9 reshape.133
  132.8 0.1 copy.57
  133.0 0.3 fusion.56
  133.3 0.1 fusion.27
  133.4 0.2 fusion.21
  133.7 0.2 fusion.1
  133.9 0.2 fusion.51
  134.1 0.2 convolution_add_fusion.1
  134.3 0.2 select_reduce_fusion
  134.5 0.1 compare_convert_fusion
  134.6 0.2 convert_reduce_fusion
  134.7 0.2 fusion.17
  134.9 0.2 fusion.8
  135.1 0.5 fusion.10
  135.6 0.5 fusion.14
  136.1 0.5 convolution_convert_fusion
  136.6 0.1 reshape.135
  136.7 0.1 copy.67
  136.8 0.7 reshape.136.refs_0_
  137.5 8.1 %exchange1.1 = bf16[8,8,768]{2,1,0:T(8,128)(2,1)} custom-call(bf16[8,8,768]{2,1,0:T(8,128)(2,1)} %reshape.136.refs_0_), custom_call_target="tpu_custom_call" | custom-call | tf_op jit(solution)/shard_map/exchange1/pallas_call | solution.py:198
  145.6 1.0 convolution_convert_fusion.6
  146.6 0.6 reshape.138
  147.2 1.3 fusion.18
  148.5 0.9 fusion.25
  149.4 0.3 fusion.20
  149.7 0.7 copy.60
  150.4 1.6 %fusion.50 = f32[4,256,256]{2,1,0:T(8,128)} fusion(f32[4,16,256]{2,1,0:T(8,128)S(1)} %fusion.10, f32[4,16,256]{2,1,0:T(8,128)S(1)} %fusion.1), kind=kOutput, calls=%fused_computation.89 | convolution fusion | flops 50413568 | bytes 1179648 | tf_op jit(solution)/shard_map/vmap(transpose(jvp()))/dot_general | solution.py:236
  152.0 1.6 %fusion.52 = f32[4,256,256]{2,1,0:T(8,128)} fusion(f32[4,16,256]{2,1,0:T(8,128)S(1)} %fusion.8, f32[4,16,256]{2,1,0:T(8,128)S(1)} %fusion.51), kind=kOutput, calls=%fused_computation.91 | convolution fusion | flops 50413568 | bytes 1179648 | tf_op jit(solution)/shard_map/vmap(transpose(jvp()))/dot_general | solution.py:238
  153.6 1.0 fusion.53
  (28 shorter events, 0.2 us)
Async XLA Ops:
  0.6 132.3 %copy-start = (bf16[4,768,256]{2,1,0:T(8,128)(2,1)S(1)}, bf16[4,768,256]{2,1,0:T(8,128)(2,1)}, u32[]{:S(2)}) copy-start(bf16[4,768,256]{2,1,0:T(8,128)(2,1)} %param.30) | copy-start | bytes 4718596
  1.9 113.8 %copy-start.8 = (s32[12,2]{0,1:T(2,128)S(1)}, s32[12,2]{0,1:T(2,128)}, u32[]{:S(2)}) copy-start(s32[12,2]{0,1:T(2,128)} %param.26) | copy-start | bytes 292
  1.9 114.4 %copy-start.5 = (bf16[12,2,56]{2,1,0:T(2,128)(2,1)S(1)}, bf16[12,2,56]{2,1,0:T(2,128)(2,1)}, u32[]{:S(2)}) copy-start(bf16[12,2,56]{2,1,0:T(2,128)(2,1)} %param.28) | copy-start | bytes 8068
  1.9 114.4 %copy-start.7 = (bf16[12,2,56]{2,1,0:T(2,128)(2,1)S(1)}, bf16[12,2,56]{2,1,0:T(2,128)(2,1)}, u32[]{:S(2)}) copy-start(bf16[12,2,56]{2,1,0:T(2,128)(2,1)} %param.27) | copy-start | bytes 8068
  114.0 19.3 %copy-start.3 = (bf16[4,56,256]{2,1,0:T(8,128)(2,1)S(1)}, bf16[4,56,256]{2,1,0:T(8,128)(2,1)}, u32[]{:S(2)}) copy-start(bf16[4,56,256]{2,1,0:T(8,128)(2,1)} %param.31) | copy-start | bytes 344068
  114.0 19.7 %copy-start.4 = (bf16[4,20,256]{2,0,1:T(4,128)(2,1)S(1)}, bf16[4,20,256]{2,0,1:T(4,128)(2,1)}, u32[]{:S(2)}) copy-start(bf16[4,20,256]{2,0,1:T(4,128)(2,1)} %param.32) | copy-start | bytes 122884
  115.7 18.2 %copy-start.1 = (bf16[4,256,256]{2,1,0:T(8,128)(2,1)S(1)}, bf16[4,256,256]{2,1,0:T(8,128)(2,1)}, u32[]{:S(2)}) copy-start(bf16[4,256,256]{2,1,0:T(8,128)(2,1)} %param.33) | copy-start | bytes 1572868
  131.8 1.4 copy-start.6
  132.9 1.2 copy-start.2
  132.9 1.4 copy-start.10
  132.9 1.8 %copy-start.9 = (bf16[4,256,56]{1,2,0:T(8,128)(2,1)S(1)}, bf16[4,256,56]{1,2,0:T(8,128)(2,1)}, u32[]{:S(2)}) copy-start(bf16[4,256,56]{1,2,0:T(8,128)(2,1)} %param.35) | copy-start | bytes 344068

commit v2 on v1

--- a/solution.py
+++ b/solution.py
@@ -254,6 +254,9 @@
 
 
 CHUNK = 64
+RING_STARTS = (0, 3, 4, 5, 6, 7)
+RING_PARTS = 2
+PUMPS = (1, 5, 5, 6, 7, 7, 8, 9, 9, 10)
 
 
 def remote(source, landing, send_sem, recv_sem, where):
@@ -273,10 +276,28 @@
     tokens,
     obs_mask,
     norm_gains,
-    joined,
+    attn_in,
+    attn_out,
     raising,
     lowering,
-    ends_out,
+    embodiment,
+    levels,
+    actions,
+    noise,
+    action_dims,
+    read_hbm,
+    act_hbm,
+    time_hbm,
+    inner_hbm,
+    outer_hbm,
+    final_hbm,
+    back_out,
+    read_out,
+    act_out,
+    time_out,
+    inner_out,
+    outer_out,
+    final_out,
     full,
     cast_rows,
     residual,
@@ -292,10 +313,10 @@
     ends_all,
     end_terms,
     out_weight,
-    z_send,
-    z_recv,
-    y_send,
-    y_recv,
+    joined,
+    returned,
+    ring_send,
+    ring_recv,
     keep_sem,
     cast_send,
     cast_recv,
@@ -307,6 +328,26 @@
     term_recv,
     mask_send,
     mask_recv,
+    read_w,
+    act_w,
+    time_w,
+    inner_w,
+    outer_w,
+    final_w,
+    turned,
+    small_out,
+    small_in,
+    rows_out,
+    rows_in,
+    back_rows,
+    back_in,
+    weight_sem,
+    small_send,
+    small_recv,
+    rows_send,
+    rows_recv,
+    back_send,
+    back_recv,
 ):
     layer_count = joined.shape[0]
     rows, model = residual.shape
@@ -316,13 +357,11 @@
     wide = model // 3
     pad = wide - width
     heads = width // HDIM
-    columns = n_dp // 2
     chunks = rows // CHUNK
+    parts = ring_send.shape[2]
     f32, bf16 = jnp.float32, jnp.bfloat16
 
     my_dp, my_mp = lax.axis_index("dp"), lax.axis_index("mp")
-    my_z, my_y = my_dp // 2, my_dp % 2
-    y_peer = {"dp": my_z * 2 + 1 - my_y}
     core = my_mp % 2
     sib = my_mp + 1 - 2 * core
     far = (my_mp + 2) % n_mp
@@ -334,14 +373,10 @@
         pl.semaphore_signal(
             barrier, inc=1, device_id={"mp": (my_mp + offset) % n_mp}, device_id_type=MESH_ID
         )
-    for offset in range(1, columns):
+    for offset in range(1, n_dp):
         pl.semaphore_signal(
-            barrier,
-            inc=1,
-            device_id={"dp": ((my_z + offset) % columns) * 2 + my_y},
-            device_id_type=MESH_ID,
-        )
-    pl.semaphore_signal(barrier, inc=1, device_id=y_peer, device_id_type=MESH_ID)
+            barrier, inc=1, device_id={"dp": (my_dp + offset) % n_dp}, device_id_type=MESH_ID
+        )
 
     def gain(index):
         return norm_gains[index : index + 1, :]
@@ -350,76 +385,103 @@
         at = pl.ds(chunk * CHUNK, CHUNK)
         cast_rows[index, my_mp, at, :] = normalize(residual[at, :], gain(gain_index)).astype(bf16)
 
+    def flipped(left, right):
+        return lax.dot_general(
+            left, right, (((0,), (0,)), ((), ())), preferred_element_type=f32
+        )
+
+    piece_row = lax.broadcasted_iota(jnp.int32, (width, model), 0)
+    piece_lane = lax.broadcasted_iota(jnp.int32, (width, model), 1)
+    picks = piece_lane == (piece_row // pad) * wide + width + piece_row % pad
+    placing = jnp.where(picks, 1.0, 0.0).astype(bf16)
+
+    def join(layer):
+        joined[layer] = flipped(attn_out[layer], placing).astype(bf16)
+        for part in range(3):
+            joined[layer, :, part * wide : part * wide + width] = attn_in[layer, part]
+
+    join(0)
     for chunk in range(chunks):
         at = pl.ds(chunk * CHUNK, CHUNK)
         residual[at, :] = tokens[at, :].astype(f32)
         norm_chunk(0, chunk, 0)
     mask_all[my_mp] = obs_mask[...]
-    pl.semaphore_wait(barrier, n_mp - 1 + columns)
+    pl.semaphore_wait(barrier, n_mp + n_dp - 2)
 
     sources = [part.at[layer] for layer in range(layer_count) for part in (joined, raising, lowering)]
 
-    def spot(unit, origin):
-        return full.at[unit, pl.ds(pl.multiple_of(origin * block, block), block)]
-
-    def z_copy(unit, offset):
+    place = ring_place(my_dp, n_dp)
+    half = n_dp // 2
+    piece = block // parts
+
+    def spot(unit, origin, part):
+        return full.at[unit, pl.ds(pl.multiple_of(origin * block + part * piece, 16), piece)]
+
+    def hop(unit, step, way, part):
+        origin = ring_index((place + (n_dp - step if way == 0 else step)) % n_dp, n_dp)
+        target = ring_index((place + (1 if way == 0 else n_dp - 1)) % n_dp, n_dp)
+        here = spot(unit, origin, part)
+        slot = step * 2 + way
         return remote(
+            sources[unit].at[pl.ds(part * piece, piece)] if step == 0 else here,
+            here,
+            ring_send.at[unit, slot, part],
+            ring_recv.at[unit, slot, part],
+            {"dp": target},
+        )
+
+    def landed(unit, step, way, part):
+        origin = ring_index(
+            (place + (n_dp - step - 1 if way == 0 else step + 1)) % n_dp, n_dp
+        )
+        here = spot(unit, origin, part)
+        slot = step * 2 + way
+        return remote(
+            here,
+            here,
+            ring_send.at[unit, slot, part],
+            ring_recv.at[unit, slot, part],
+            {"dp": ring_index((place + (1 if way == 0 else n_dp - 1)) % n_dp, n_dp)},
+        )
+
+    def legs(step):
+        return [
+            (way, part)
+            for part in range(parts)
+            for way in range(2)
+            if step < half - 1 or (part < (parts + 1) // 2) == (way == 0)
+        ]
+
+    def kept(unit):
+        return pltpu.make_async_copy(
             sources[unit],
-            spot(unit, my_dp),
-            z_send.at[unit, offset],
-            z_recv.at[unit, offset],
-            {"dp": ((my_z + offset) % columns) * 2 + my_y},
-        )
-
-    def z_landed(unit, offset):
-        origin = ((my_z + columns - offset) % columns) * 2 + my_y
-        return remote(
-            sources[unit],
-            spot(unit, origin),
-            z_send.at[unit, offset],
-            z_recv.at[unit, offset],
-            {"dp": origin},
-        )
-
-    def y_copy(unit, offset):
-        origin = ((my_z + columns - offset) % columns) * 2 + my_y
-        return remote(
-            sources[unit] if offset == 0 else spot(unit, origin),
-            spot(unit, origin),
-            y_send.at[unit, offset],
-            y_recv.at[unit, offset],
-            y_peer,
-        )
-
-    def y_landed(unit, offset):
-        origin = ((my_z + columns - offset) % columns) * 2 + 1 - my_y
-        return remote(
-            sources[unit],
-            spot(unit, origin),
-            y_send.at[unit, offset],
-            y_recv.at[unit, offset],
-            y_peer,
-        )
-
-    def kept(unit):
-        return pltpu.make_async_copy(sources[unit], spot(unit, my_dp), keep_sem.at[unit])
-
-    def z_start(unit):
-        for offset in range(1, columns):
-            z_copy(unit, offset).start()
-        kept(unit).start()
-
-    def relay(unit, offset):
-        z_landed(unit, offset).wait_recv()
-        y_copy(unit, offset).start()
-
-    def relay_all(unit):
-        for offset in range(1, columns):
-            relay(unit, offset)
+            full.at[unit, pl.ds(pl.multiple_of(my_dp * block, block), block)],
+            keep_sem.at[unit],
+        )
+
+    def tick(now):
+        for unit in range(len(sources)):
+            step = now - (RING_STARTS[unit])
+            if step == 0:
+                for way, part in legs(0):
+                    hop(unit, 0, way, part).start()
+                kept(unit).start()
+            elif 0 < step <= half:
+                after = legs(step) if step < half else []
+                for way, part in legs(step - 1):
+                    landed(unit, step - 1, way, part).wait_recv()
+                    if (way, part) in after:
+                        hop(unit, step, way, part).start()
+
+    clock = [0]
+
+    def pump(until):
+        while clock[0] <= until:
+            tick(clock[0])
+            clock[0] += 1
 
     def complete(unit):
-        for offset in range(columns):
-            y_landed(unit, offset).wait_recv()
+        pump(RING_STARTS[unit] + half)
         kept(unit).wait()
 
     def cast_copy(index, way, chunk):
@@ -531,21 +593,108 @@
             obs_mask, mask_all.at[my_mp], mask_send.at[offset], mask_recv.at[offset], who
         )
 
-    z_start(0)
-    y_copy(0, 0).start()
+    def swap_copy(source, landing, send_sem, recv_sem, offset):
+        peer = (my_dp + offset) % n_dp
+        return remote(
+            source.at[peer],
+            landing.at[my_dp],
+            send_sem.at[offset],
+            recv_sem.at[offset],
+            {"dp": peer},
+        )
+
+    def swap_landed(source, landing, send_sem, recv_sem, offset):
+        peer = (my_dp + n_dp - offset) % n_dp
+        return remote(
+            source.at[peer],
+            landing.at[peer],
+            send_sem.at[offset],
+            recv_sem.at[offset],
+            {"dp": peer},
+        )
+
+    def swap_start(*swap):
+        for offset in range(1, n_dp):
+            swap_copy(*swap, offset).start()
+        swap[1][my_dp] = swap[0][my_dp]
+
+    def swap_wait(*swap):
+        for offset in range(1, n_dp):
+            swap_landed(*swap, offset).wait_recv()
+
+    small_swap = (small_out, small_in, small_send, small_recv)
+    rows_swap = (rows_out, rows_in, rows_send, rows_recv)
+    back_swap = (back_rows, back_in, back_send, back_recv)
+    head_count, slot_rows = read_hbm.shape[0], rows_in.shape[1]
+    all_rows = n_dp * slot_rows
+    weight_copies = [
+        pltpu.make_async_copy(source, landing, weight_sem.at[index])
+        for index, (source, landing) in enumerate(
+            (
+                (read_hbm, read_w),
+                (act_hbm, act_w),
+                (time_hbm, time_w),
+                (inner_hbm, inner_w),
+                (outer_hbm, outer_w),
+                (final_hbm, final_w),
+            )
+        )
+    ]
+
+    pump(0)
     for offset, who in peers():
         mask_copy(offset, who).start()
     for chunk in range(chunks):
         cast_copy(0, 1, chunk).start()
         cast_copy(0, 0, chunk).start()
-    z_start(1)
-    for step in range(max(chunks, columns - 1)):
-        if step < chunks:
-            cast_pass(0, step)
-        if step < columns - 1:
-            relay(0, step + 1)
-    y_copy(1, 0).start()
-    z_start(2)
+    for copy in weight_copies:
+        copy.start()
+    join(1)
+    group = levels.shape[1]
+    act = actions.shape[2]
+    tile = 128
+    slots = ends_all.shape[1]
+    end_rows = n_mp * slots
+    slot_of = lax.broadcasted_iota(jnp.int32, (all_rows, group), 0)
+    sample_at = lax.broadcasted_iota(jnp.int32, (group, end_rows), 0)
+    end_of = lax.broadcasted_iota(jnp.int32, (group, end_rows), 1)
+    end_sample = (end_of // slots) * samples + end_of % slots // READ
+    end_here = (end_sample == sample_at) & (end_of % slots < samples * READ)
+    square = lax.broadcasted_iota(jnp.int32, (group, group), 0)
+    square = square == lax.broadcasted_iota(jnp.int32, (group, group), 1)
+    level_lane = lax.broadcasted_iota(jnp.int32, (group, tile), 1)
+    table_lane = lax.broadcasted_iota(jnp.int32, (1, tile), 1)
+    table = jnp.zeros((1, tile), f32)
+    for level, value in enumerate(plan_values()):
+        table = jnp.where(table_lane == level, value, table)
+    spread = jnp.zeros((all_rows, end_rows), f32)
+    scattered = [jnp.zeros((all_rows, act), f32)] * 2 + [jnp.zeros((all_rows, tile), f32)]
+    clean_all, noise_all = actions[...].astype(f32), noise[...].astype(f32)
+    for read in range(READ):
+        route = (embodiment[...] == slot_of // READ) & (slot_of % READ == read)
+        route = jnp.where(route, 1.0, 0.0).astype(bf16)
+        ends_here = jnp.where(end_here & (end_of % READ == read), 1.0, 0.0).astype(bf16)
+        spread = spread + dot32(route, ends_here)
+        level = jnp.sum(
+            jnp.where(square, levels[read : read + 1, :], 0), axis=1, keepdims=True
+        )
+        onehot = jnp.where(level_lane == level, 1.0, 0.0)
+        kept_share = jnp.sum(onehot * table, axis=1, keepdims=True)
+        clean, drawn = clean_all[:, read, :], noise_all[:, read, :]
+        mixed = jnp.sqrt(kept_share) * clean + jnp.sqrt(1.0 - kept_share) * drawn
+        for index, values in enumerate((mixed, drawn, onehot)):
+            scattered[index] = scattered[index] + dot32(route, values.astype(bf16))
+    spread = spread.astype(bf16)
+    small_out[...] = jnp.zeros(small_out.shape, bf16)
+    for peer in range(n_dp):
+        at = slice(peer * slot_rows, (peer + 1) * slot_rows)
+        for index, values in enumerate(scattered):
+            columns = slice(index * tile, index * tile + values.shape[1])
+            small_out[peer, :, columns] = values[at].astype(bf16)
+    swap_start(*small_swap)
+    for chunk in range(chunks):
+        cast_pass(0, chunk)
+        pump(PUMPS[0] + chunk)
 
     lane = lax.broadcasted_iota(jnp.int32, (1, wide), 1)
     lane_masks = [
@@ -628,21 +777,22 @@
     take_out_weight(0)
     pair_rows(near_first, lambda owner: project(0, 0, owner))
     pair_rows(far_first, lambda owner: project(0, 0, owner))
+    pump(PUMPS[1])
     attention(0)
+    pump(PUMPS[2])
 
     def attended(owner):
         at = pl.ds(pl.multiple_of(owner * rows, rows), rows)
         return dot_turned(context[at, :], out_weight[...])
 
     def after_attention():
-        relay_all(1)
-        y_copy(2, 0).start()
-        z_start(3)
+        pump(PUMPS[3])
 
     combine(0, attended, after_attention)
     sum_finish(0, 1, 1)
     for chunk in range(chunks):
         cast_pass(1, chunk)
+    pump(PUMPS[4])
     complete(1)
 
     def raise_rows(owner):
@@ -652,9 +802,7 @@
 
     cast_near(1)
     pair_rows(near_first, raise_rows)
-    relay_all(2)
-    y_copy(3, 0).start()
-    z_start(4)
+    pump(PUMPS[5])
     cast_far(1)
     pair_rows(far_first, raise_rows)
     complete(2)
@@ -663,9 +811,7 @@
         return dot_turned(hidden[owner], full[2])
 
     def after_mlp():
-        relay_all(3)
-        y_copy(4, 0).start()
-        z_start(5)
+        pump(PUMPS[6])
 
     combine(1, lowered_rows, after_mlp)
     sum_finish(1, 2, 2)
@@ -677,17 +823,17 @@
         ends_copy(offset, who).start()
     for chunk in range(chunks):
         cast_pass(2, chunk)
+    pump(PUMPS[7])
     complete(3)
     take_out_weight(3)
     cast_near(2)
     pair_rows(near_first, lambda owner: project(2, 3, owner))
-    relay_all(4)
-    y_copy(5, 0).start()
+    pump(PUMPS[8])
     cast_far(2)
     pair_rows(far_first, lambda owner: project(2, 3, owner))
     attention(16)
-
-    slots = ends_all.shape[1]
+    pump(PUMPS[9])
+
     row = lax.broadcasted_iota(jnp.int32, (n_mp * slots, n_mp * samples * 16), 0)
     col = lax.broadcasted_iota(jnp.int32, (n_mp * slots, n_mp * samples * 16), 1)
     inner = row % slots
@@ -716,7 +862,6 @@
             ends_recv.at[offset],
             who,
         ).wait_recv()
-    relay_all(5)
     ends = jnp.concatenate([ends_all[owner] for owner in range(n_mp)], axis=0)
     ends = gathered_terms(0, ends)
     normed = normalize(ends, gain(3)).astype(bf16)
@@ -725,13 +870,90 @@
     complete(5)
     share(1, dot_turned(raised, full[5]))
     ends = gathered_terms(1, ends)
-    ends_out[...] = normalize(ends, gain(4)).astype(bf16)
+    readouts = normalize(ends, gain(4)).astype(bf16)
+
+    scattered = dot32(spread, readouts)
+    for peer in range(n_dp):
+        rows_out[peer] = scattered[peer * slot_rows : (peer + 1) * slot_rows].astype(bf16)
+    swap_start(*rows_swap)
+    for copy in weight_copies:
+        copy.wait()
+    swap_wait(*small_swap)
+    facts = jnp.concatenate([small_in[peer].astype(f32) for peer in range(n_dp)], axis=0)
+    noisy = facts[:, :tile].astype(bf16)
+    target = facts[:, tile : tile + act]
+    onehot = facts[:, 2 * tile :].astype(bf16)
+    row_of = lax.broadcasted_iota(jnp.int32, (all_rows, act), 0) % slot_rows // READ
+    live = jnp.sum(facts[:, 2 * tile :], axis=1, keepdims=True)
+    column = lax.broadcasted_iota(jnp.int32, (1, act), 1) % ADIM_MAX
+    times = time_w[...].astype(f32)
+    firsts = [
+        dot32(noisy[:, :act], act_w[head]) + dot32(onehot[:, :LEVELS], times[:, head, :].astype(bf16))
+        for head in range(head_count)
+    ]
+    swap_wait(*rows_swap)
+    features = jnp.concatenate([rows_in[peer].astype(f32) for peer in range(n_dp)], axis=0)
+    features = features.astype(bf16)
+
+    def slope(value):
+        gate = jax.nn.sigmoid(value)
+        return gate * (1.0 + value * (1.0 - gate))
+
+    kept_back = []
+    backward = jnp.zeros((all_rows, model), f32)
+    for head in range(head_count):
+        first = firsts[head] + dot32(features, read_w[head])
+        active = jax.nn.silu(first).astype(bf16)
+        inner = dot32(active, inner_w[head])
+        second = jax.nn.silu(inner).astype(bf16)
+        above = first + dot32(second, outer_w[head])
+        third = jax.nn.silu(above).astype(bf16)
+        predicted = dot_turned(third, final_w[head])
+        slot = my_dp * head_count + head
+        dims = jnp.where(slot < EMB, action_dims[jnp.minimum(slot, EMB - 1)], 0)
+        mask = jnp.where((row_of == head) & (column < dims), live, 0.0)
+        differ = (mask * (predicted - target)).astype(bf16)
+        above_grad = dot32(differ, final_w[head]).astype(bf16).astype(f32) * slope(above)
+        above_bf = above_grad.astype(bf16)
+        inner_grad = dot_turned(above_bf, outer_w[head]).astype(bf16).astype(f32) * slope(inner)
+        inner_bf = inner_grad.astype(bf16)
+        first_grad = above_grad + dot_turned(inner_bf, inner_w[head]).astype(bf16).astype(
+            f32
+        ) * slope(first)
+        first_bf = first_grad.astype(bf16)
+        backward = backward + dot_turned(first_bf, read_w[head])
+        kept_back.append((active, second, third, differ, above_bf, inner_bf, first_bf))
+    for peer in range(n_dp):
+        back_rows[peer] = backward[peer * slot_rows : (peer + 1) * slot_rows].astype(bf16)
+    swap_start(*back_swap)
+
+    turned[...] = jnp.transpose(features.astype(f32)).astype(bf16)
+    own_features = turned[pl.ds(pl.multiple_of(my_mp * width, 16), width), :]
+    for head, kept_now in enumerate(kept_back):
+        active, second, third, differ, above_bf, inner_bf, first_bf = kept_now
+        read_out[head] = dot32(own_features, first_bf)
+        act_out[head] = flipped(noisy, first_bf)[:act]
+        time_out[:, head, :] = flipped(onehot, first_bf)[:LEVELS]
+        inner_out[head] = flipped(active, inner_bf)
+        outer_out[head] = flipped(second, above_bf)
+        final_out[head] = flipped(differ, third)
+    swap_wait(*back_swap)
+    arrived = jnp.concatenate([back_in[peer].astype(f32) for peer in range(n_dp)], axis=0)
+    arrived = flipped(spread, arrived.astype(bf16))
+    for owner in range(n_mp):
+        returned[owner] = arrived[owner * slots : (owner + 1) * slots]
+    mine = returned[my_mp]
+    for sample in range(samples):
+        back_out[sample] = mine[READ * sample : READ * (sample + 1)].astype(bf16)
 
     for unit in range(len(sources)):
-        for offset in range(columns):
-            if offset:
-                z_copy(unit, offset).wait_send()
-            y_copy(unit, offset).wait_send()
+        for step in range(half):
+            for way, part in legs(step):
+                hop(unit, step, way, part).wait_send()
+    for offset in range(1, n_dp):
+        swap_copy(*small_swap, offset).wait_send()
+        swap_copy(*rows_swap, offset).wait_send()
+        swap_copy(*back_swap, offset).wait_send()
     for index in range(3):
         for way in range(3):
             for chunk in range(chunks):
@@ -749,22 +971,53 @@
             term_copy(index, offset, who).wait_send()
 
 
-def trunk(tokens, obs_mask, norm_gains, joined, raising, lowering):
+def plan_values():
+    anchor = math.cos(0.008 / 1.008 * math.pi / 2) ** 2
+    steps = [(level + 1.0) / LEVELS for level in range(LEVELS)]
+    return [math.cos((up + 0.008) / 1.008 * math.pi / 2) ** 2 / anchor for up in steps]
+
+
+def trunk(
+    tokens,
+    obs_mask,
+    norm_gains,
+    attn_in,
+    attn_out,
+    raising,
+    lowering,
+    embodiment,
+    levels,
+    actions,
+    noise,
+    action_dims,
+    *head_weights,
+):
     n_dp, n_mp = lax.axis_size("dp"), lax.axis_size("mp")
     rows, model = tokens.shape
     samples = obs_mask.shape[0]
     wide = model // 3
-    units = 3 * joined.shape[0]
-    columns, chunks = n_dp // 2, rows // CHUNK
+    units = 3 * raising.shape[0]
+    chunks = rows // CHUNK
+    parts = RING_PARTS if raising.shape[1] % (16 * RING_PARTS) == 0 else 1
     slots = samples * READ + (-samples * READ) % 8
+    heads = head_weights[0].shape[0]
     bf16, f32 = jnp.bfloat16, jnp.float32
     dma = pltpu.SemaphoreType.DMA
     vmem = pltpu.VMEM
+    inner_spec = pl.BlockSpec(memory_space=vmem)
+    outer_spec = pl.BlockSpec(memory_space=pl.ANY)
+    grads = []
+    for index, weight in enumerate(head_weights):
+        shape = weight.shape if index else (heads, model // n_mp, weight.shape[2])
+        grads.append(jax.ShapeDtypeStruct(shape, f32))
+    per_owner = heads * READ
     return pl.pallas_call(
         functools.partial(trunk_kernel, n_dp, n_mp),
-        out_shape=jax.ShapeDtypeStruct((n_mp * slots, model), bf16),
-        in_specs=[pl.BlockSpec(memory_space=vmem)] * 6,
-        out_specs=pl.BlockSpec(memory_space=vmem),
+        out_shape=[jax.ShapeDtypeStruct((samples, READ, model), bf16)] + grads,
+        in_specs=[inner_spec] * 11
+        + [pl.BlockSpec(memory_space=pltpu.SMEM)]
+        + [outer_spec] * len(head_weights),
+        out_specs=[inner_spec] * (1 + len(grads)),
         scratch_shapes=[
             vmem((units, model, model), bf16),
             vmem((3, n_mp, rows, model), bf16),
@@ -781,10 +1034,10 @@
             vmem((n_mp, slots, model), f32),
             vmem((2, n_mp, n_mp * slots, model), bf16),
             vmem((model, wide), bf16),
-            dma((units, columns)),
-            dma((units, columns)),
-            dma((units, columns)),
-            dma((units, columns)),
+            vmem(raising.shape, bf16),
+            vmem((n_mp, slots, model), f32),
+            dma((units, n_dp, parts)),
+            dma((units, n_dp, parts)),
             dma((units,)),
             dma((3, 3, chunks)),
             dma((3, 3, chunks)),
@@ -796,10 +1049,30 @@
             dma((2, n_mp)),
             dma((n_mp,)),
             dma((n_mp,)),
-        ],
+        ]
+        + [vmem(weight.shape, weight.dtype) for weight in head_weights]
+        + [vmem((model, n_dp * per_owner), bf16)]
+        + [vmem((n_dp, per_owner, 3 * 128), bf16)] * 2
+        + [vmem((n_dp, per_owner, model), bf16)] * 4
+        + [dma((len(head_weights),))]
+        + [dma((n_dp,))] * 6,
         compiler_params=pltpu.CompilerParams(collective_id=50, has_side_effects=True),
         name="trunk",
-    )(tokens, obs_mask, norm_gains, joined, raising, lowering)
+    )(
+        tokens,
+        obs_mask,
+        norm_gains,
+        attn_in,
+        attn_out,
+        raising,
+        lowering,
+        embodiment,
+        levels,
+        actions,
+        noise,
+        action_dims,
+        *head_weights,
+    )
 
 
 def general_trunk(ident, tokens, obs_mask, norm_gains, attn_in, attn_out, mlp_in, mlp_out, small):
@@ -895,23 +1168,51 @@
     return normalize(ends, norm_gains[2 * layer_count]).astype(jnp.bfloat16), got_small
 
 
-def fused_trunk(ident, tokens, obs_mask, norm_gains, attn_in, attn_out, mlp_in, mlp_out, small):
-    model = tokens.shape[1]
-    width = attn_in.shape[3]
-    pad = model // 3 - width
-    samples_local = obs_mask.shape[0]
-    n_mp = lax.axis_size("mp")
-    pieces = []
-    turned = jnp.swapaxes(attn_out, 1, 2)
-    for part in range(3):
-        pieces += [attn_in[:, part], turned[:, :, part * pad : (part + 1) * pad]]
-    joined = jnp.concatenate(pieces, axis=2)
-    ends = trunk(tokens, obs_mask, norm_gains, joined, mlp_in, jnp.swapaxes(mlp_out, 1, 2))
-    ends = ends.reshape(n_mp, -1, model)[:, : samples_local * READ]
-    return ends.reshape(-1, model), None
-
-
-def fits_fused(tokens, obs_mask, attn_in, mlp_in):
+def fused(
+    tokens,
+    obs_mask,
+    norm_gains,
+    attn_in,
+    attn_out,
+    mlp_in,
+    mlp_out,
+    embodiment,
+    levels,
+    actions,
+    noise,
+    action_dims,
+    head_read,
+    head_act,
+    time_table,
+    block_in,
+    block_out,
+    head_out,
+):
+    outs = trunk(
+        tokens,
+        obs_mask,
+        norm_gains,
+        attn_in,
+        attn_out,
+        mlp_in,
+        jnp.swapaxes(mlp_out, 1, 2),
+        embodiment.T,
+        levels.T,
+        actions,
+        noise,
+        action_dims,
+        head_read,
+        head_act,
+        jnp.swapaxes(time_table, 0, 1),
+        block_in,
+        block_out,
+        jnp.swapaxes(head_out, 1, 2),
+    )
+    back, read, act, times, inner, outer, final = outs
+    return back, read, act, jnp.swapaxes(times, 0, 1), inner, outer, jnp.swapaxes(final, 1, 2)
+
+
+def fits_fused(tokens, obs_mask, attn_in, mlp_in, head_read, actions):
     n_mp, n_dp = lax.axis_size("mp"), lax.axis_size("dp")
     model, width = tokens.shape[1], attn_in.shape[3]
     pad = model // 3 - width
@@ -925,6 +1226,8 @@
         and 3 * pad == width
         and tokens.shape[0] % CHUNK == 0
         and obs_mask.shape[1] == CHUNK
+        and head_read.shape[0] * READ == 8
+        and actions.shape[2] <= 128
     )
 
 
@@ -948,6 +1251,27 @@
     block_out,
     head_out,
 ):
+    if fits_fused(tokens, obs_mask, attn_in, mlp_in, head_read, actions):
+        return fused(
+            tokens,
+            obs_mask,
+            norm_gains,
+            attn_in,
+            attn_out,
+            mlp_in,
+            mlp_out,
+            embodiment,
+            levels,
+            actions,
+            noise,
+            action_dims,
+            head_read,
+            head_act,
+            time_table,
+            block_in,
+            block_out,
+            head_out,
+        )
     model = tokens.shape[1]
     act = actions.shape[2]
     samples_local = obs_mask.shape[0]
@@ -976,16 +1300,12 @@
     small = dot32(spread_rows, small).astype(jnp.bfloat16)
     small = small.reshape(n_dp, heads_dev * READ, small.shape[1])
 
-    run = fused_trunk if fits_fused(tokens, obs_mask, attn_in, mlp_in) else general_trunk
-    readouts, got_small = run(
+    readouts, got_small = general_trunk(
         ident, tokens, obs_mask, norm_gains, attn_in, attn_out, mlp_in, mlp_out, small
     )
     send = dot32(spread_rows, readouts).astype(jnp.bfloat16)
     send = send.reshape(n_dp, heads_dev * READ, model)
-    if got_small is None:
-        got_features, got_small = exchange(next(ident), ("swap", send), ("swap", small))
-    else:
-        (got_features,) = exchange(next(ident), ("swap", send))
+    (got_features,) = exchange(next(ident), ("swap", send))
 
     def by_head(values):
         values = values.reshape(n_dp, heads_dev, READ, values.shape[-1])

time: 155 us -> 129 us (0.83)
  matrix products: 12.3 us -> 0 us
  Pallas kernels: 132 us -> 120 us
  other arithmetic: 1.94 us -> 0 us
    dot_general x19 -> x0, matrix products: 12.3 us -> none  [the longest x3 2.32 us: tail(): jnp.dot(active, inner_weight, preferred_element_type=jnp.float32, precisi...]
    pallas_call x3 -> x1, Pallas kernels: 132 us -> 120 us  [trunk(): pl.pallas_call(functools.partial(trunk_kernel, n_dp, n_mp), out_shape=[ja...]
    unnamed x25 -> x17, local copies, waits for them, and re-layouts: 1.83 us -> 7.44 us
    reshape x8 -> x0, local copies, waits for them, and re-layouts: 3.51 us -> none  [the longest x1 0.94 us: by_head(): values = values.reshape(n_dp, heads_dev, READ, values.shape[-1])]
where the time goes in v2:
time: 129 us; the launch traced here: 128 us
  Pallas kernels  120 us (93%)
  local copies, waits for them, and re-layouts  7.44 us (6%)
    pallas_call x1, Pallas kernels, trunk(): pl.pallas_call(functools.partial(trunk_kernel, n_dp, n_mp), out_shape=[ja...  120 us
    unnamed x17, local copies, waits for them, and re-layouts  7.44 us

profile of v2, /device:TPU:0, one launch (start us, length us, event | category | flops | bytes accessed | tf_op | source)
XLA Modules:
  0.0 128.4 jit_solution(10021437036570076902)
XLA Ops:
  0.6 120.2 %trunk.1 = (bf16[3,2,768]{2,1,0:T(2,128)(2,1)}, f32[4,192,256]{2,1,0:T(8,128)}, f32[4,56,256]{2,1,0:T(8,128)}, f32[20,4,256]{2,1,0:T(4,128)}, f32[4,256,256]{2,1...) custom-call(bf16[192,768]{1,0:T(8,128)(2,1)} %tokens.1, s32[3,64]{1,0:T(4,128)} %obs_mask.1, ...), custom_call_target="tpu_custom_call" | custom-call | tf_op jit(solution)/shard_map/trunk/pallas_call | solution.py:1014
  120.9 0.0 copy-start.3
  120.9 0.0 copy-start.4
  120.9 0.0 copy-start.1
  120.9 1.4 %copy.32 = bf16[3,2,768]{2,1,0:T(2,128)(2,1)} copy(bf16[3,2,768]{2,1,0:T(2,128)(2,1)} %get-tuple-element.28) | data formatting | bytes 18432
  122.3 2.1 %copy.33 = f32[4,192,256]{2,1,0:T(8,128)} copy(f32[4,192,256]{2,1,0:T(8,128)} %get-tuple-element.29) | data formatting | bytes 1572864
  124.4 0.0 copy-done.3
  124.4 0.0 copy-start
  124.4 0.7 copy.34
  125.1 0.0 copy-done.4
  125.1 0.6 copy.35
  125.7 0.0 copy-done.1
  125.7 0.0 copy-start.2
  125.7 1.0 copy.36
  126.7 0.0 copy-done
  126.7 1.0 copy.37
  127.7 0.0 copy-done.2
  127.7 0.7 copy.38
Async XLA Ops:
  120.9 3.5 %copy-start.3 = (f32[4,56,256]{2,1,0:T(8,128)S(1)}, f32[4,56,256]{2,1,0:T(8,128)}, u32[]{:S(2)}) copy-start(f32[4,56,256]{2,1,0:T(8,128)} %get-tuple-element.30) | copy-start | bytes 688132
  120.9 4.2 %copy-start.4 = (f32[20,4,256]{2,1,0:T(4,128)S(1)}, f32[20,4,256]{2,1,0:T(4,128)}, u32[]{:S(2)}) copy-start(f32[20,4,256]{2,1,0:T(4,128)} %get-tuple-element.17) | copy-start | bytes 245764
  120.9 4.8 %copy-start.1 = (f32[4,256,256]{2,1,0:T(8,128)S(1)}, f32[4,256,256]{2,1,0:T(8,128)}, u32[]{:S(2)}) copy-start(f32[4,256,256]{2,1,0:T(8,128)} %get-tuple-element.32) | copy-start | bytes 3145732
  124.4 2.3 %copy-start = (f32[4,256,256]{2,1,0:T(8,128)S(1)}, f32[4,256,256]{2,1,0:T(8,128)}, u32[]{:S(2)}) copy-start(f32[4,256,256]{2,1,0:T(8,128)} %get-tuple-element.33) | copy-start | bytes 3145732
  125.7 1.9 %copy-start.2 = (f32[4,56,256]{2,1,0:T(8,128)S(1)}, f32[4,56,256]{2,1,0:T(8,128)}, u32[]{:S(2)}) copy-start(f32[4,56,256]{2,1,0:T(8,128)} %get-tuple-element.20) | copy-start | bytes 688132

commit v3 on v2

--- a/solution.py
+++ b/solution.py
@@ -254,9 +254,9 @@
 
 
 CHUNK = 64
-RING_STARTS = (0, 3, 4, 5, 6, 7)
+RING_STARTS = (0, 2, 4, 5, 6, 7)
 RING_PARTS = 2
-PUMPS = (1, 5, 5, 6, 7, 7, 8, 9, 9, 10)
+PUMPS = (1, 1, 2, 2, 7, 7, 9, 9, 10, 13, 13, 14, 14, 16, 17, 17, 18, 20, 21, 22, 23, 23, 24, 25, 26, 27, 27, 28, 29)
 
 
 def remote(source, landing, send_sem, recv_sem, where):
@@ -459,29 +459,30 @@
             keep_sem.at[unit],
         )
 
-    def tick(now):
-        for unit in range(len(sources)):
-            step = now - (RING_STARTS[unit])
+    events = sorted(
+        (RING_STARTS[unit] + step, unit, step)
+        for unit in range(len(sources))
+        for step in range(half + 1)
+    )
+    done = [0]
+
+    def pump(count):
+        while done[0] < min(count, len(events)):
+            _, unit, step = events[done[0]]
+            done[0] += 1
             if step == 0:
                 for way, part in legs(0):
                     hop(unit, 0, way, part).start()
                 kept(unit).start()
-            elif 0 < step <= half:
-                after = legs(step) if step < half else []
-                for way, part in legs(step - 1):
-                    landed(unit, step - 1, way, part).wait_recv()
-                    if (way, part) in after:
-                        hop(unit, step, way, part).start()
-
-    clock = [0]
-
-    def pump(until):
-        while clock[0] <= until:
-            tick(clock[0])
-            clock[0] += 1
+                continue
+            after = legs(step) if step < half else []
+            for way, part in legs(step - 1):
+                landed(unit, step - 1, way, part).wait_recv()
+                if (way, part) in after:
+                    hop(unit, step, way, part).start()
 
     def complete(unit):
-        pump(RING_STARTS[unit] + half)
+        pump(events.index((RING_STARTS[unit] + half, unit, half)) + 1)
         kept(unit).wait()
 
     def cast_copy(index, way, chunk):
@@ -569,6 +570,7 @@
             norm_chunk(next_cast, chunk, gain_index)
             cast_copy(next_cast, 1, chunk).start()
             cast_copy(next_cast, 0, chunk).start()
+            pump(PUMPS[(9, 19)[index] + chunk])
 
     def peers():
         return [(offset, {"mp": (my_mp + offset) % n_mp}) for offset in range(1, n_mp)]
@@ -641,7 +643,7 @@
         )
     ]
 
-    pump(0)
+    pump(PUMPS[0])
     for offset, who in peers():
         mask_copy(offset, who).start()
     for chunk in range(chunks):
@@ -694,7 +696,7 @@
     swap_start(*small_swap)
     for chunk in range(chunks):
         cast_pass(0, chunk)
-        pump(PUMPS[0] + chunk)
+        pump(PUMPS[1 + chunk])
 
     lane = lax.broadcasted_iota(jnp.int32, (1, wide), 1)
     lane_masks = [
@@ -765,6 +767,7 @@
         partial_rows[far] = part_of(far).astype(bf16)
         partial_rows[sib] = part_of(sib).astype(bf16)
         sum_own(index).start()
+        pump(PUMPS[(7, 17)[index]])
         sum_cross(index)
         residual[...] = residual[...] + part_of(my_mp)
         late()
@@ -776,23 +779,24 @@
         mask_copy(offset, who).wait_recv()
     take_out_weight(0)
     pair_rows(near_first, lambda owner: project(0, 0, owner))
+    pump(PUMPS[4])
     pair_rows(far_first, lambda owner: project(0, 0, owner))
-    pump(PUMPS[1])
+    pump(PUMPS[5])
     attention(0)
-    pump(PUMPS[2])
+    pump(PUMPS[6])
 
     def attended(owner):
         at = pl.ds(pl.multiple_of(owner * rows, rows), rows)
         return dot_turned(context[at, :], out_weight[...])
 
     def after_attention():
-        pump(PUMPS[3])
+        pump(PUMPS[8])
 
     combine(0, attended, after_attention)
     sum_finish(0, 1, 1)
     for chunk in range(chunks):
         cast_pass(1, chunk)
-    pump(PUMPS[4])
+        pump(PUMPS[12 + chunk])
     complete(1)
 
     def raise_rows(owner):
@@ -802,16 +806,17 @@
 
     cast_near(1)
     pair_rows(near_first, raise_rows)
-    pump(PUMPS[5])
+    pump(PUMPS[15])
     cast_far(1)
     pair_rows(far_first, raise_rows)
+    pump(PUMPS[16])
     complete(2)
 
     def lowered_rows(owner):
         return dot_turned(hidden[owner], full[2])
 
     def after_mlp():
-        pump(PUMPS[6])
+        pump(PUMPS[18])
 
     combine(1, lowered_rows, after_mlp)
     sum_finish(1, 2, 2)
@@ -823,16 +828,17 @@
         ends_copy(offset, who).start()
     for chunk in range(chunks):
         cast_pass(2, chunk)
-    pump(PUMPS[7])
+        pump(PUMPS[22 + chunk])
     complete(3)
     take_out_weight(3)
     cast_near(2)
     pair_rows(near_first, lambda owner: project(2, 3, owner))
-    pump(PUMPS[8])
+    pump(PUMPS[25])
     cast_far(2)
     pair_rows(far_first, lambda owner: project(2, 3, owner))
+    pump(PUMPS[26])
     attention(16)
-    pump(PUMPS[9])
+    pump(PUMPS[27])
 
     row = lax.broadcasted_iota(jnp.int32, (n_mp * slots, n_mp * samples * 16), 0)
     col = lax.broadcasted_iota(jnp.int32, (n_mp * slots, n_mp * samples * 16), 1)
@@ -854,6 +860,7 @@
         return ends
 
     share(0, dot_turned(ends_context, out_weight[...]))
+    pump(PUMPS[28])
     for offset, who in peers():
         remote(
             ends_all.at[my_mp],

time: 129 us -> 116 us (0.90)
  Pallas kernels: 120 us -> 108 us
    pallas_call x1, Pallas kernels: 120 us -> 108 us  [trunk(): pl.pallas_call(functools.partial(trunk_kernel, n_dp, n_mp), out_shape=[ja...]
where the time goes in v3:
time: 116 us
  Pallas kernels  108 us (93%)
  local copies, waits for them, and re-layouts  7.44 us (6%)
    pallas_call x1, Pallas kernels, trunk(): pl.pallas_call(functools.partial(trunk_kernel, n_dp, n_mp), out_shape=[ja...  108 us
    unnamed x17, local copies, waits for them, and re-layouts  7.44 us

profile of v3, /device:TPU:0, one launch (start us, length us, event | category | flops | bytes accessed | tf_op | source)
XLA Modules:
  0.0 116.0 jit_solution(1094439251185895628)
XLA Ops:
  0.6 107.9 %trunk.1 = (bf16[3,2,768]{2,1,0:T(2,128)(2,1)}, f32[4,192,256]{2,1,0:T(8,128)}, f32[4,56,256]{2,1,0:T(8,128)}, f32[20,4,256]{2,1,0:T(4,128)}, f32[4,256,256]{2,1...) custom-call(bf16[192,768]{1,0:T(8,128)(2,1)} %tokens.1, s32[3,64]{1,0:T(4,128)} %obs_mask.1, ...), custom_call_target="tpu_custom_call" | custom-call | tf_op jit(solution)/shard_map/trunk/pallas_call | solution.py:1021
  108.5 0.0 copy-start.3
  108.5 0.0 copy-start.4
  108.6 0.0 copy-start.1
  108.6 1.4 %copy.32 = bf16[3,2,768]{2,1,0:T(2,128)(2,1)} copy(bf16[3,2,768]{2,1,0:T(2,128)(2,1)} %get-tuple-element.28) | data formatting | bytes 18432
  110.0 2.1 %copy.33 = f32[4,192,256]{2,1,0:T(8,128)} copy(f32[4,192,256]{2,1,0:T(8,128)} %get-tuple-element.29) | data formatting | bytes 1572864
  112.0 0.0 copy-done.3
  112.0 0.0 copy-start
  112.0 0.7 copy.34
  112.7 0.0 copy-done.4
  112.7 0.6 copy.35
  113.4 0.0 copy-done.1
  113.4 0.0 copy-start.2
  113.4 1.0 copy.36
  114.3 0.0 copy-done
  114.3 1.0 copy.37
  115.3 0.0 copy-done.2
  115.3 0.7 copy.38
Async XLA Ops:
  108.5 3.5 %copy-start.3 = (f32[4,56,256]{2,1,0:T(8,128)S(1)}, f32[4,56,256]{2,1,0:T(8,128)}, u32[]{:S(2)}) copy-start(f32[4,56,256]{2,1,0:T(8,128)} %get-tuple-element.30) | copy-start | bytes 688132
  108.5 4.2 %copy-start.4 = (f32[20,4,256]{2,1,0:T(4,128)S(1)}, f32[20,4,256]{2,1,0:T(4,128)}, u32[]{:S(2)}) copy-start(f32[20,4,256]{2,1,0:T(4,128)} %get-tuple-element.17) | copy-start | bytes 245764
  108.6 4.8 %copy-start.1 = (f32[4,256,256]{2,1,0:T(8,128)S(1)}, f32[4,256,256]{2,1,0:T(8,128)}, u32[]{:S(2)}) copy-start(f32[4,256,256]{2,1,0:T(8,128)} %get-tuple-element.32) | copy-start | bytes 3145732
  112.0 2.3 %copy-start = (f32[4,256,256]{2,1,0:T(8,128)S(1)}, f32[4,256,256]{2,1,0:T(8,128)}, u32[]{:S(2)}) copy-start(f32[4,256,256]{2,1,0:T(8,128)} %get-tuple-element.33) | copy-start | bytes 3145732
  113.4 1.9 %copy-start.2 = (f32[4,56,256]{2,1,0:T(8,128)S(1)}, f32[4,56,256]{2,1,0:T(8,128)}, u32[]{:S(2)}) copy-start(f32[4,56,256]{2,1,0:T(8,128)} %get-tuple-element.20) | copy-start | bytes 688132
